TPU v7x, 256 devices: a whole 4x4x8 slice. The times are simulated.
256 devices in a mesh: gx: 16 (over z_lo, x, core), gy: 4 (over y), gz: 4 (over z_hi).
Axes of the slice: x: 4, y: 4, z: 8 (z_hi: 4, z_lo: 2; z = z_hi * 2 + z_lo), core: 2. Of those that a mesh axis runs over, the one named last changes fastest.
Arguments:
- estimate: float32 [384, 128, 512], P('gx', 'gy', 'gz'), may hold values from 0.03 to 11, as said below
- view_images: float32 [4, 384, 128, 512], P(None, 'gx', 'gy', 'gz'), may hold values from 0.015 to 21, as said below
- psf_taps: int32 [4, 3, 31], replicated, may hold values from 1 to 64
- view_weights: int32 [4], replicated, may hold values from 1 to 4
Outputs:
- deconvolved: float32 [384, 128, 512], P('gx', 'gy', 'gz')
- misfit: float32 [2, 4], replicated
Inputs may be any that keep to these rules, and one draw needn't show every extreme that they name: `estimate`: positive. `view_images`: positive.
All inputs are finite; a program needn't handle non-finite values.
Results may differ from a plain program's by a relative error of at most 0.0001.
Values sent between devices are 32-bit elements; how exact they have to be, the bound alone decides.
No kernel may reach another device: no remote copies, remote signals or barrier semaphores. Data moves between devices by JAX's collectives and lax.ppermute only.
A program may use at most 128 MiB of HBM per device.

v0:
```python
import functools

import jax
import jax.numpy as jnp
from jax import lax
from jax.sharding import Mesh
from jax.sharding import PartitionSpec as P

TAPS = 31
ITERS = 2
GX_GY_GZ = ("gx_0", "gx_1", "gx_2", "gy", "gz")
GX = ("gx_0", "gx_1", "gx_2")


def one_axis_at_a_time(shard, axes):
    return functools.reduce(lax.psum, axes, shard)


def extended(block, sides, width):
    for axis, dim in sides:
        count = lax.axis_size(axis)
        forward = [(i, i + 1) for i in range(count - 1)]
        backward = [(target, source) for source, target in forward]
        low = lax.ppermute(
            lax.slice_in_dim(block, block.shape[dim] - width, None, axis=dim), axis, forward
        )
        high = lax.ppermute(lax.slice_in_dim(block, 0, width, axis=dim), axis, backward)
        block = jnp.concatenate([low, block, high], axis=dim)
    return block


def toeplitz(kernels, length):
    span = kernels.shape[-1]
    offsets = jnp.arange(length + span - 1)[:, None] - jnp.arange(length)[None, :]
    indicator = (offsets[:, :, None] == jnp.arange(span)[None, None, :]).astype(jnp.float32)
    return jnp.einsum("vt,jit->vji", kernels, indicator, precision=lax.Precision.HIGHEST)


def product(form, left, right):
    return jnp.einsum(form, left, right, precision=lax.Precision.HIGHEST)


def local(estimate, view_images, psf_taps, view_weights):
    halo_width = (TAPS - 1) // 2
    cells_x, cells_y, cells_z = estimate.shape
    kernels = psf_taps.astype(jnp.float32) / 256.0
    flipped = kernels[:, :, ::-1]
    forward_x = toeplitz(kernels[:, 0], cells_x)
    forward_y = toeplitz(kernels[:, 1], cells_y)
    forward_z = toeplitz(kernels[:, 2], cells_z)
    backward_x = toeplitz(flipped[:, 0], cells_x)
    backward_y = toeplitz(flipped[:, 1], cells_y)
    backward_z = toeplitz(flipped[:, 2], cells_z)
    tap_sums = jnp.sum(kernels, axis=2)
    weight_float = view_weights.astype(jnp.float32)
    normalizer = jnp.sum(weight_float * jnp.prod(tap_sums, axis=1))
    backward_z = backward_z * (weight_float / normalizer)[:, None, None]
    data_total, data_square = (
        one_axis_at_a_time(jnp.sum(view_images, axis=(1, 2, 3)), GX_GY_GZ),
        one_axis_at_a_time(jnp.sum(view_images * view_images, axis=(1, 2, 3)), GX_GY_GZ),
    )
    misfits = []
    for iteration in range(ITERS):
        padded = extended(estimate, ((GX, 0),), halo_width)
        partial_value = product("jyz,vji->viyz", padded, forward_x)
        padded = extended(partial_value, (("gy", 2),), halo_width)
        partial_value = product("vxjz,vji->vxiz", padded, forward_y)
        padded = extended(partial_value, (("gz", 3),), halo_width)
        blurred = product("vxyj,vji->vxyi", padded, forward_z)
        local_total = jnp.sum(blurred, axis=(1, 2, 3))
        blurred_total, cross_total, blurred_square = (
            one_axis_at_a_time(local_total, GX_GY_GZ),
            one_axis_at_a_time(jnp.sum(view_images * blurred, axis=(1, 2, 3)), GX_GY_GZ),
            one_axis_at_a_time(jnp.sum(blurred * blurred, axis=(1, 2, 3)), GX_GY_GZ),
        )
        flux_scale = data_total / blurred_total
        scaled = flux_scale[:, None, None, None] * blurred
        squared = (
            data_square - 2.0 * flux_scale * cross_total + flux_scale * flux_scale * blurred_square
        )
        misfits.append(squared / data_square)
        quotient = view_images / scaled
        padded = extended(quotient, ((GX, 1),), halo_width)
        partial_value = product("vjyz,vji->viyz", padded, backward_x)
        padded = extended(partial_value, (("gy", 2),), halo_width)
        partial_value = product("vxjz,vji->vxiz", padded, backward_y)
        padded = extended(partial_value, (("gz", 3),), halo_width)
        correction = product("vxyj,vji->xyi", padded, backward_z)
        estimate = estimate * correction
    return (estimate, jnp.stack(misfits))


def solution(mesh):
    torus = Mesh(
        mesh.devices.reshape(2, 4, 2, mesh.shape["gy"], mesh.shape["gz"]),
        ("gx_0", "gx_1", "gx_2", "gy", "gz"),
    )
    in_specs = (P(GX, "gy", "gz"), P(None, GX, "gy", "gz"), P(), P())
    out_specs = (P(GX, "gy", "gz"), P())
    return jax.shard_map(local, mesh=torus, in_specs=in_specs, out_specs=out_specs, check_vma=False)
```

profile of v0, /device:TPU:34, one launch (start us, length us, event | category | flops | bytes accessed | tf_op | source)
XLA Modules:
  0.0 487.0 jit_solution(7171152705583981746)
XLA Ops:
  1.9 1.9 collective-permute-start
  3.8 3.6 collective-permute-start.1
  12.9 3.5 collective-permute-start.2
  18.0 14.4 %collective-permute-done.2 = f32[4,24,15,128]{3,1,2,0:T(8,128)S(1)} collective-permute-done((f32[4,24,15,128]{3,1,2,0:T(8,128)S(1)}, f32[4,24,15,128]{3,1,2,0:T(8,128)S(1)}, u32[]{:S(2)}, u32[]{:S(2)}) %collective-permute-start.2) | collective-permute-done | bytes 737312 | tf_op jit(solution)/shard_map/ppermute | solution.py:24
  32.4 4.7 collective-permute-done.3
  37.3 2.2 fusion.38
  41.3 3.0 copy.36
  44.2 6.0 %collective-permute-start.4 = (f32[4,24,32,15]{2,1,3,0:T(8,128)}, f32[4,24,32,15]{2,1,3,0:T(8,128)}, u32[]{:S(2)}, u32[]{:S(2)}) collective-permute-start(f32[4,24,32,15]{2,1,3,0:T(8,128)} %copy.36), channel_id=1, source_target_pairs={{0,1},{1,2},{2,3},{4,5},{5,6},{6,7},{8,9},{9,10},{10,11},{12,13},{... | collective-permute-start | bytes 552968 | tf_op jit(solution)/shard_map/ppermute | solution.py:24
  54.7 26.7 %collective-permute-done.4 = f32[4,24,32,15]{2,1,3,0:T(8,128)} collective-permute-done((f32[4,24,32,15]{2,1,3,0:T(8,128)}, f32[4,24,32,15]{2,1,3,0:T(8,128)}, u32[]{:S(2)}, u32[]{:S(2)}) %collective-permute-start.4) | collective-permute-done | bytes 184352 | tf_op jit(solution)/shard_map/ppermute | solution.py:24
  81.4 2.9 copy.38
  84.3 3.0 copy.39
  87.3 7.1 %multiply_reduce_fusion.3 = (f32[4]{0:T(128)S(1)}, f32[4]{0:T(128)S(1)}, f32[4]{0:T(128)S(1)}, f32[4]{0:T(128)}, f32[4]{0:T(128)S(1)}, /*index=5*/f32[4,24,32,128]{3,2,1,0:T(8,128)}) fusion(f32[4,24,32,128]{3,2,1,0:T(8,128)S(1)} %copy-done, f32[4,158,128,1]{2,0,1,3:T(4,128)S(1)} %fusion.64, f32[4,24,32,15]{3,2,1,0:T(8,128)} %copy.39, ...), kind=kOutput, calls=%fused_computation.48 | convolution fusion | flops 749654016 | bytes 5410896 | tf_op jit(solution)/shard_map/vxyj,vji->vxyi/dot_general | solution.py:40
  94.4 9.2 %all-reduce.9 = (f32[4]{0:T(128)S(1)}, f32[4]{0:T(128)S(1)}) all-reduce(f32[4]{0:T(128)S(1)} %get-tuple-element.6, f32[4]{0:T(128)S(1)} %get-tuple-element.4), channel_id=1, replica_groups=mesh['gx_0'=2,'gx_1'=4,'gx_2'=2,'gy'=4,'gz'=4] {'gx_0'}, use_global_device_ids=true, to_apply=%region_1.0 | all-reduce | flops 8 | bytes 64 | tf_op jit(solution)/shard_map/psum | solution.py:16
  103.6 8.7 %all-reduce.5 = (f32[4]{0:T(128)S(1)}, f32[4]{0:T(128)S(1)}) all-reduce(f32[4]{0:T(128)S(1)} %get-tuple-element.48, f32[4]{0:T(128)S(1)} %get-tuple-element.49), channel_id=1, replica_groups=mesh['gx_0'=2,'gx_1'=4,'gx_2'=2,'gy'=4,'gz'=4] {'gx_1'}, use_global_device_ids=true, to_apply=%region_2.0 | all-reduce | flops 8 | bytes 64 | tf_op jit(solution)/shard_map/psum | solution.py:16
  112.3 2.5 all-reduce.7
  114.7 9.2 %all-reduce.3 = (f32[4]{0:T(128)S(1)}, f32[4]{0:T(128)S(1)}) all-reduce(f32[4]{0:T(128)S(1)} %get-tuple-element.40, f32[4]{0:T(128)S(1)} %get-tuple-element.41), channel_id=1, replica_groups=mesh['gx_0'=2,'gx_1'=4,'gx_2'=2,'gy'=4,'gz'=4] {'gy'}, use_global_device_ids=true, to_apply=%region_4.0 | all-reduce | flops 8 | bytes 64 | tf_op jit(solution)/shard_map/psum | solution.py:16
  124.0 13.0 %all-reduce.1 = (f32[4]{0:T(128)S(1)}, f32[4]{0:T(128)S(1)}) all-reduce(f32[4]{0:T(128)S(1)} %get-tuple-element.24, f32[4]{0:T(128)S(1)} %get-tuple-element.25), channel_id=1, replica_groups=mesh['gx_0'=2,'gx_1'=4,'gx_2'=2,'gy'=4,'gz'=4] {'gz'}, use_global_device_ids=true, to_apply=%region_5.0 | all-reduce | flops 8 | bytes 64 | tf_op jit(solution)/shard_map/psum | solution.py:16
  142.4 3.6 collective-permute-start.7
  146.4 9.8 %collective-permute-done.6 = f32[4,15,32,128]{3,2,1,0:T(8,128)} collective-permute-done((f32[4,15,32,128]{3,2,1,0:T(8,128)}, f32[4,15,32,128]{3,2,1,0:T(8,128)}, u32[]{:S(2)}, u32[]{:S(2)}) %collective-permute-start.6) | collective-permute-done | bytes 983072 | tf_op jit(solution)/shard_map/ppermute | solution.py:24
  159.8 3.9 fusion.2
  164.9 3.4 collective-permute-start.8
  170.5 13.3 %collective-permute-done.8 = f32[4,24,15,128]{3,1,2,0:T(8,128)} collective-permute-done((f32[4,24,15,128]{3,1,2,0:T(8,128)}, f32[4,24,15,128]{3,1,2,0:T(8,128)}, u32[]{:S(2)}, u32[]{:S(2)}) %collective-permute-start.8) | collective-permute-done | bytes 737312 | tf_op jit(solution)/shard_map/ppermute | solution.py:24
  183.8 5.0 %collective-permute-done.9 = f32[4,24,15,128]{3,1,2,0:T(8,128)} collective-permute-done((f32[4,24,15,128]{3,1,2,0:T(8,128)}, f32[4,24,15,128]{3,1,2,0:T(8,128)}, u32[]{:S(2)}, u32[]{:S(2)}) %collective-permute-start.9) | collective-permute-done | bytes 737312 | tf_op jit(solution)/shard_map/ppermute | solution.py:27
  190.4 2.2 fusion.41
  192.5 2.2 fusion.104
  194.8 2.9 copy.45
  197.7 2.7 collective-permute-start.10
  200.4 3.0 copy.46
  207.0 23.5 %collective-permute-done.10 = f32[4,24,32,15]{2,1,3,0:T(8,128)} collective-permute-done((f32[4,24,32,15]{2,1,3,0:T(8,128)}, f32[4,24,32,15]{2,1,3,0:T(8,128)}, u32[]{:S(2)}, u32[]{:S(2)}) %collective-permute-start.10) | collective-permute-done | bytes 184352 | tf_op jit(solution)/shard_map/ppermute | solution.py:24
  230.6 2.9 copy.47
  233.5 2.9 copy.48
  236.4 5.7 %fusion.58 = f32[24,32,128]{2,1,0:T(8,128)S(1)} fusion(f32[24,32,128]{2,1,0:T(8,128)} %param.4, f32[4,24,32,15]{3,2,1,0:T(8,128)} %copy.48, f32[4,24,32,128]{3,2,1,0:T(8,128)S(1)} %fusion.41, f32[4,24,32,15]{3,2,1,0:T(8,128)} %copy.47, f32[4,158,128,1]{2,0,1,3:T(4,128)} %fusion.66), kind=kOutput, calls=%fused_computation.60 | convolution fusion | flops 746606592 | bytes 3051520 | tf_op jit(solution)/shard_map/vxyj,vji->xyi/dot_general | solution.py:40
  244.0 3.6 collective-permute-start.13
  247.7 1.9 collective-permute-done.12
  256.4 14.0 %collective-permute-done.14 = f32[4,24,15,128]{3,1,2,0:T(8,128)S(1)} collective-permute-done((f32[4,24,15,128]{3,1,2,0:T(8,128)S(1)}, f32[4,24,15,128]{3,1,2,0:T(8,128)S(1)}, u32[]{:S(2)}, u32[]{:S(2)}) %collective-permute-start.14) | collective-permute-done | bytes 737312 | tf_op jit(solution)/shard_map/ppermute | solution.py:24
  270.4 4.9 collective-permute-done.15
  275.5 2.2 fusion.44
  277.7 2.2 fusion.102
  279.9 2.9 copy.55
  282.8 13.2 %collective-permute-start.16 = (f32[4,24,32,15]{2,1,3,0:T(8,128)}, f32[4,24,32,15]{2,1,3,0:T(8,128)}, u32[]{:S(2)}, u32[]{:S(2)}) collective-permute-start(f32[4,24,32,15]{2,1,3,0:T(8,128)} %copy.55), channel_id=1, source_target_pairs={{0,1},{1,2},{2,3},{4,5},{5,6},{6,7},{8,9},{9,10},{10,11},{12,13},{... | collective-permute-start | bytes 552968 | tf_op jit(solution)/shard_map/ppermute | solution.py:24
  296.1 3.0 copy.56
  300.5 27.1 %collective-permute-done.16 = f32[4,24,32,15]{2,1,3,0:T(8,128)} collective-permute-done((f32[4,24,32,15]{2,1,3,0:T(8,128)}, f32[4,24,32,15]{2,1,3,0:T(8,128)}, u32[]{:S(2)}, u32[]{:S(2)}) %collective-permute-start.16) | collective-permute-done | bytes 184352 | tf_op jit(solution)/shard_map/ppermute | solution.py:24
  327.7 2.9 copy.57
  330.6 5.4 %collective-permute-done.17 = f32[4,24,32,15]{2,1,3,0:T(8,128)} collective-permute-done((f32[4,24,32,15]{2,1,3,0:T(8,128)}, f32[4,24,32,15]{2,1,3,0:T(8,128)}, u32[]{:S(2)}, u32[]{:S(2)}) %collective-permute-start.17) | collective-permute-done | bytes 184352 | tf_op jit(solution)/shard_map/ppermute | solution.py:27
  335.9 2.9 copy.58
  338.9 7.0 %multiply_reduce_fusion.1 = (f32[4]{0:T(128)S(1)}, f32[4]{0:T(128)}, f32[4]{0:T(128)}, f32[4,24,32,128]{3,2,1,0:T(8,128)}) fusion(f32[4,24,32,128]{3,2,1,0:T(8,128)S(1)} %copy-done, f32[4,158,128,1]{2,0,1,3:T(4,128)} %copy-done.1, f32[4,24,32,15]{3,2,1,0:T(8,128)} %copy.58, f32[4,24,32,128]{3,2,1,0:T(8,128)S(1)} %fusion.44, f32[4,24,32,15]{3,2,1,0:T(8,128)} %copy.57), kind=kOutput, calls=%fused_computation.46 | convolution fusion | flops 748474368 | bytes 5410864 | tf_op jit(solution)/shard_map/vxyj,vji->vxyi/dot_general | solution.py:40
  345.9 5.1 %all-reduce.8 = (f32[4]{0:T(128)S(1)}, f32[4]{0:T(128)S(1)}, f32[4]{0:T(128)S(1)}, f32[4]{0:T(128)S(1)}, f32[4]{0:T(128)S(1)}, /*index=5*/f32[4]{0:T(128)S(1)}) all-reduce(f32[4]{0:T(128)} %get-tuple-element.9, f32[4]{0:T(128)S(1)} %copy-done.13, ...), channel_id=1, replica_groups=mesh['gx_0'=2,'gx_1'=4,'gx_2'=2,'gy'=4,'gz'=4] {'gx_0'}, use_global_device_ids=true, to_apply=%region_16.0 | all-reduce | flops 24 | bytes 192 | tf_op jit(solution)/shard_map/psum | solution.py:16
  351.0 6.9 %all-reduce.4 = (f32[4]{0:T(128)S(1)}, f32[4]{0:T(128)S(1)}, f32[4]{0:T(128)S(1)}, f32[4]{0:T(128)S(1)}, f32[4]{0:T(128)S(1)}, /*index=5*/f32[4]{0:T(128)S(1)}) all-reduce(f32[4]{0:T(128)S(1)} %get-tuple-element.42, f32[4]{0:T(128)S(1)} %get-tuple-element.43, ...), channel_id=1, replica_groups=mesh['gx_0'=2,'gx_1'=4,'gx_2'=2,'gy'=4,'gz'=4] {'gx_1'}, use_global_device_ids=true, to_apply=%region_17.0 | all-reduce | flops 24 | bytes 192 | tf_op jit(solution)/shard_map/psum | solution.py:16
  357.9 2.5 all-reduce.6
  360.3 8.3 %all-reduce.2 = (f32[4]{0:T(128)S(1)}, f32[4]{0:T(128)S(1)}, f32[4]{0:T(128)S(1)}, f32[4]{0:T(128)S(1)}, f32[4]{0:T(128)S(1)}, /*index=5*/f32[4]{0:T(128)S(1)}) all-reduce(f32[4]{0:T(128)S(1)} %get-tuple-element.34, f32[4]{0:T(128)S(1)} %get-tuple-element.35, ...), channel_id=1, replica_groups=mesh['gx_0'=2,'gx_1'=4,'gx_2'=2,'gy'=4,'gz'=4] {'gy'}, use_global_device_ids=true, to_apply=%region_19.0 | all-reduce | flops 24 | bytes 192 | tf_op jit(solution)/shard_map/psum | solution.py:16
  368.6 9.9 %all-reduce = (f32[4]{0:T(128)S(1)}, f32[4]{0:T(128)S(1)}, f32[4]{0:T(128)S(1)}, f32[4]{0:T(128)S(1)}, f32[4]{0:T(128)S(1)}, /*index=5*/f32[4]{0:T(128)S(1)}) all-reduce(f32[4]{0:T(128)S(1)} %get-tuple-element.18, f32[4]{0:T(128)S(1)} %get-tuple-element.19, ...), channel_id=1, replica_groups=mesh['gx_0'=2,'gx_1'=4,'gx_2'=2,'gy'=4,'gz'=4] {'gz'}, use_global_device_ids=true, to_apply=%region_20.0 | all-reduce | flops 24 | bytes 192 | tf_op jit(solution)/shard_map/psum | solution.py:16
  383.2 3.8 collective-permute-start.19
  387.0 9.7 %collective-permute-done.18 = f32[4,15,32,128]{3,2,1,0:T(8,128)S(1)} collective-permute-done((f32[4,15,32,128]{3,2,1,0:T(8,128)S(1)}, f32[4,15,32,128]{3,2,1,0:T(8,128)S(1)}, u32[]{:S(2)}, u32[]{:S(2)}) %collective-permute-start.18) | collective-permute-done | bytes 983072 | tf_op jit(solution)/shard_map/ppermute | solution.py:24
  399.0 3.9 fusion
  403.0 3.1 collective-permute-start.20
  407.8 13.9 %collective-permute-done.20 = f32[4,24,15,128]{3,1,2,0:T(8,128)S(1)} collective-permute-done((f32[4,24,15,128]{3,1,2,0:T(8,128)S(1)}, f32[4,24,15,128]{3,1,2,0:T(8,128)S(1)}, u32[]{:S(2)}, u32[]{:S(2)}) %collective-permute-start.20) | collective-permute-done | bytes 737312 | tf_op jit(solution)/shard_map/ppermute | solution.py:24
  421.7 4.9 collective-permute-done.21
  426.8 2.2 fusion.47
  430.7 3.0 copy.64
  433.7 5.1 %collective-permute-start.22 = (f32[4,24,32,15]{2,1,3,0:T(8,128)}, f32[4,24,32,15]{2,1,3,0:T(8,128)}, u32[]{:S(2)}, u32[]{:S(2)}) collective-permute-start(f32[4,24,32,15]{2,1,3,0:T(8,128)} %copy.64), channel_id=1, source_target_pairs={{0,1},{1,2},{2,3},{4,5},{5,6},{6,7},{8,9},{9,10},{10,11},{12,13},{... | collective-permute-start | bytes 552968 | tf_op jit(solution)/shard_map/ppermute | solution.py:24
  442.1 27.6 %collective-permute-done.22 = f32[4,24,32,15]{2,1,3,0:T(8,128)} collective-permute-done((f32[4,24,32,15]{2,1,3,0:T(8,128)}, f32[4,24,32,15]{2,1,3,0:T(8,128)}, u32[]{:S(2)}, u32[]{:S(2)}) %collective-permute-start.22) | collective-permute-done | bytes 184352 | tf_op jit(solution)/shard_map/ppermute | solution.py:24
  471.5 6.3 %collective-permute-done.23 = f32[4,24,32,15]{2,1,3,0:T(8,128)} collective-permute-done((f32[4,24,32,15]{2,1,3,0:T(8,128)}, f32[4,24,32,15]{2,1,3,0:T(8,128)}, u32[]{:S(2)}, u32[]{:S(2)}) %collective-permute-start.23) | collective-permute-done | bytes 184352 | tf_op jit(solution)/shard_map/ppermute | solution.py:27
  477.8 2.9 copy.67
  480.7 5.8 %fusion.61 = f32[24,32,128]{2,1,0:T(8,128)} fusion(f32[24,32,128]{2,1,0:T(8,128)S(1)} %fusion.58, f32[4,24,32,15]{3,2,1,0:T(8,128)} %copy.67, f32[4,24,32,128]{3,2,1,0:T(8,128)S(1)} %fusion.47, f32[4,24,32,15]{3,2,1,0:T(8,128)S(1)} %copy.66, f32[4,158,128,1]{2,0,1,3:T(4,128)} %fusion.66), kind=kOutput, calls=%fused_computation.61 | convolution fusion | flops 746606592 | bytes 3051520 | tf_op jit(solution)/shard_map/vxyj,vji->xyi/dot_general | solution.py:40
  (99 shorter events, 58.6 us)
Async XLA Ops:
  0.6 6.9 %copy-start.12 = (s32[4,3,31]{2,0,1:T(4,128)S(1)}, s32[4,3,31]{2,0,1:T(4,128)}, u32[]{:S(2)}) copy-start(s32[4,3,31]{2,0,1:T(4,128)} %param.6) | copy-start | bytes 4468
  1.9 7.7 %collective-permute-start = (f32[15,32,128]{2,0,1:T(8,128)S(1)}, f32[15,32,128]{2,0,1:T(8,128)S(1)}, u32[]{:S(2)}, u32[]{:S(2)}) collective-permute-start(f32[15,32,128]{2,0,1:T(8,128)S(1)} %get-tuple-element.74), channel_id=1, source_target_pairs={{0,16},{16,32},{32,48},{48,64},{64,80},{80,96},{96,112},{112,128},... | collective-permute-start | bytes 737288 | tf_op jit(solution)/shard_map/ppermute | solution.py:24
  3.8 7.5 %collective-permute-start.1 = (f32[15,32,128]{2,0,1:T(8,128)S(1)}, f32[15,32,128]{2,0,1:T(8,128)S(1)}, u32[]{:S(2)}, u32[]{:S(2)}) collective-permute-start(f32[15,32,128]{2,0,1:T(8,128)S(1)} %get-tuple-element.75), channel_id=1, source_target_pairs={{16,0},{32,16},{48,32},{64,48},{80,64},{96,80},{112,96},{128,112},... | collective-permute-start | bytes 737288 | tf_op jit(solution)/shard_map/ppermute | solution.py:27
  7.8 3.5 copy-start.8
  12.9 19.6 %collective-permute-start.2 = (f32[4,24,15,128]{3,1,2,0:T(8,128)S(1)}, f32[4,24,15,128]{3,1,2,0:T(8,128)S(1)}, u32[]{:S(2)}, u32[]{:S(2)}) collective-permute-start(f32[4,24,15,128]{3,1,2,0:T(8,128)S(1)} %get-tuple-element.70), channel_id=1, source_target_pairs={{0,4},{4,8},{8,12},{1,5},{5,9},{9,13},{2,6},{6,10},{10,14},{3,7},{... | collective-permute-start | bytes 2211848 | tf_op jit(solution)/shard_map/ppermute | solution.py:24
  16.4 20.7 %collective-permute-start.3 = (f32[4,24,15,128]{3,1,2,0:T(8,128)S(1)}, f32[4,24,15,128]{3,1,2,0:T(8,128)S(1)}, u32[]{:S(2)}, u32[]{:S(2)}) collective-permute-start(f32[4,24,15,128]{3,1,2,0:T(8,128)S(1)} %get-tuple-element.71), channel_id=1, source_target_pairs={{4,0},{8,4},{12,8},{5,1},{9,5},{13,9},{6,2},{10,6},{14,10},{7,3},{... | collective-permute-start | bytes 2211848 | tf_op jit(solution)/shard_map/ppermute | solution.py:27
  18.0 19.3 %copy-start.4 = (f32[4,62,32,1]{1,0,2,3:T(4,128)}, f32[4,62,32,1]{1,0,2,3:T(4,128)S(1)}, u32[]{:S(2)}) copy-start(f32[4,62,32,1]{1,0,2,3:T(4,128)S(1)} %convolution_bitcast_fusion) | copy-start | bytes 95236
  44.2 37.1 %collective-permute-start.4 = (f32[4,24,32,15]{2,1,3,0:T(8,128)}, f32[4,24,32,15]{2,1,3,0:T(8,128)}, u32[]{:S(2)}, u32[]{:S(2)}) collective-permute-start(f32[4,24,32,15]{2,1,3,0:T(8,128)} %copy.36), channel_id=1, source_target_pairs={{0,1},{1,2},{2,3},{4,5},{5,6},{6,7},{8,9},{9,10},{10,11},{12,13},{... | collective-permute-start | bytes 552968 | tf_op jit(solution)/shard_map/ppermute | solution.py:24
  51.8 32.4 %collective-permute-start.5 = (f32[4,24,32,15]{2,1,3,0:T(8,128)}, f32[4,24,32,15]{2,1,3,0:T(8,128)}, u32[]{:S(2)}, u32[]{:S(2)}) collective-permute-start(f32[4,24,32,15]{2,1,3,0:T(8,128)} %copy.37), channel_id=1, source_target_pairs={{1,0},{2,1},{3,2},{5,4},{6,5},{7,6},{9,8},{10,9},{11,10},{13,12},{... | collective-permute-start | bytes 552968 | tf_op jit(solution)/shard_map/ppermute | solution.py:27
  53.1 0.6 copy-start.10
  54.7 32.6 %copy-start.1 = (f32[4,158,128,1]{2,0,1,3:T(4,128)}, f32[4,158,128,1]{2,0,1,3:T(4,128)S(1)}, u32[]{:S(2)}) copy-start(f32[4,158,128,1]{2,0,1,3:T(4,128)S(1)} %fusion.64) | copy-start | bytes 970756
  84.3 3.0 copy-start
  137.0 1.8 copy-start.15
  137.0 1.8 copy-start.14
  140.4 15.7 %collective-permute-start.6 = (f32[4,15,32,128]{3,2,1,0:T(8,128)}, f32[4,15,32,128]{3,2,1,0:T(8,128)}, u32[]{:S(2)}, u32[]{:S(2)}) collective-permute-start(f32[4,15,32,128]{3,2,1,0:T(8,128)} %get-tuple-element.66), channel_id=1, source_target_pairs={{0,16},{16,32},{32,48},{48,64},{64,80},{80,96},{96,112},{112,128},... | collective-permute-start | bytes 2949128 | tf_op jit(solution)/shard_map/ppermute | solution.py:24
  142.4 15.6 %collective-permute-start.7 = (f32[4,15,32,128]{3,2,1,0:T(8,128)}, f32[4,15,32,128]{3,2,1,0:T(8,128)}, u32[]{:S(2)}, u32[]{:S(2)}) collective-permute-start(f32[4,15,32,128]{3,2,1,0:T(8,128)} %get-tuple-element.67), channel_id=1, source_target_pairs={{16,0},{32,16},{48,32},{64,48},{80,64},{96,80},{112,96},{128,112},... | collective-permute-start | bytes 2949128 | tf_op jit(solution)/shard_map/ppermute | solution.py:27
  146.4 13.4 %copy-start.6 = (f32[4,54,24,1]{1,0,2,3:T(4,128)}, f32[4,54,24,1]{1,0,2,3:T(4,128)S(1)}, u32[]{:S(2)}) copy-start(f32[4,54,24,1]{1,0,2,3:T(4,128)S(1)} %convolution_bitcast_fusion.3) | copy-start | bytes 62212
  163.7 6.0 %copy-start.16 = (s32[4]{0:T(128)S(1)}, s32[4]{0:T(128)}, u32[]{:S(2)}) copy-start(s32[4]{0:T(128)} %param.7) | copy-start | bytes 52
  164.9 18.9 %collective-permute-start.8 = (f32[4,24,15,128]{3,1,2,0:T(8,128)}, f32[4,24,15,128]{3,1,2,0:T(8,128)}, u32[]{:S(2)}, u32[]{:S(2)}) collective-permute-start(f32[4,24,15,128]{3,1,2,0:T(8,128)} %get-tuple-element.64), channel_id=1, source_target_pairs={{0,4},{4,8},{8,12},{1,5},{5,9},{9,13},{2,6},{6,10},{10,14},{3,7},{... | collective-permute-start | bytes 2211848 | tf_op jit(solution)/shard_map/ppermute | solution.py:24
  168.4 20.5 %collective-permute-start.9 = (f32[4,24,15,128]{3,1,2,0:T(8,128)}, f32[4,24,15,128]{3,1,2,0:T(8,128)}, u32[]{:S(2)}, u32[]{:S(2)}) collective-permute-start(f32[4,24,15,128]{3,1,2,0:T(8,128)} %get-tuple-element.65), channel_id=1, source_target_pairs={{4,0},{8,4},{12,8},{5,1},{9,5},{13,9},{6,2},{10,6},{14,10},{7,3},{... | collective-permute-start | bytes 2211848 | tf_op jit(solution)/shard_map/ppermute | solution.py:27
  170.5 19.8 %copy-start.2 = (f32[4,62,32,1]{1,0,2,3:T(4,128)}, f32[4,62,32,1]{1,0,2,3:T(4,128)S(1)}, u32[]{:S(2)}) copy-start(f32[4,62,32,1]{1,0,2,3:T(4,128)S(1)} %convolution_bitcast_fusion.1) | copy-start | bytes 95236
  197.7 7.1 %copy-start.17 = (s32[4]{0:T(128)S(1)}, s32[4]{0:T(128)}, u32[]{:S(2)}) copy-start(s32[4]{0:T(128)} %param.7) | copy-start | bytes 52
  197.7 7.7 %copy-start.11 = (s32[158,128]{1,0:T(8,128)S(1)}, s32[158,128]{1,0:T(8,128)}, u32[]{:S(2)}) copy-start(s32[158,128]{1,0:T(8,128)} %copy-done.10) | copy-start | bytes 242692
  197.7 32.8 %collective-permute-start.10 = (f32[4,24,32,15]{2,1,3,0:T(8,128)}, f32[4,24,32,15]{2,1,3,0:T(8,128)}, u32[]{:S(2)}, u32[]{:S(2)}) collective-permute-start(f32[4,24,32,15]{2,1,3,0:T(8,128)} %copy.45), channel_id=1, source_target_pairs={{0,1},{1,2},{2,3},{4,5},{5,6},{6,7},{8,9},{9,10},{10,11},{12,13},{... | collective-permute-start | bytes 552968 | tf_op jit(solution)/shard_map/ppermute | solution.py:24
  203.3 30.1 %collective-permute-start.11 = (f32[4,24,32,15]{2,1,3,0:T(8,128)}, f32[4,24,32,15]{2,1,3,0:T(8,128)}, u32[]{:S(2)}, u32[]{:S(2)}) collective-permute-start(f32[4,24,32,15]{2,1,3,0:T(8,128)} %copy.46), channel_id=1, source_target_pairs={{1,0},{2,1},{3,2},{5,4},{6,5},{7,6},{9,8},{10,9},{11,10},{13,12},{... | collective-permute-start | bytes 552968 | tf_op jit(solution)/shard_map/ppermute | solution.py:27
  242.0 9.4 %copy-start.9 = (f32[4,54,24,1]{1,0,2,3:T(4,128)S(1)}, f32[4,54,24,1]{1,0,2,3:T(4,128)}, u32[]{:S(2)}) copy-start(f32[4,54,24,1]{1,0,2,3:T(4,128)} %copy-done.8) | copy-start | bytes 62212
  242.1 7.5 %collective-permute-start.12 = (f32[15,32,128]{2,1,0:T(8,128)S(1)}, f32[15,32,128]{2,1,0:T(8,128)S(1)}, u32[]{:S(2)}, u32[]{:S(2)}) collective-permute-start(f32[15,32,128]{2,1,0:T(8,128)S(1)} %get-tuple-element.72), channel_id=1, source_target_pairs={{0,16},{16,32},{32,48},{48,64},{64,80},{80,96},{96,112},{112,128},... | collective-permute-start | bytes 737288 | tf_op jit(solution)/shard_map/ppermute | solution.py:24
  244.0 7.3 %collective-permute-start.13 = (f32[15,32,128]{2,1,0:T(8,128)S(1)}, f32[15,32,128]{2,1,0:T(8,128)S(1)}, u32[]{:S(2)}, u32[]{:S(2)}) collective-permute-start(f32[15,32,128]{2,1,0:T(8,128)S(1)} %get-tuple-element.73), channel_id=1, source_target_pairs={{16,0},{32,16},{48,32},{64,48},{80,64},{96,80},{112,96},{128,112},... | collective-permute-start | bytes 737288 | tf_op jit(solution)/shard_map/ppermute | solution.py:27
  253.4 17.0 %collective-permute-start.14 = (f32[4,24,15,128]{3,1,2,0:T(8,128)S(1)}, f32[4,24,15,128]{3,1,2,0:T(8,128)S(1)}, u32[]{:S(2)}, u32[]{:S(2)}) collective-permute-start(f32[4,24,15,128]{3,1,2,0:T(8,128)S(1)} %get-tuple-element.60), channel_id=1, source_target_pairs={{0,4},{4,8},{8,12},{1,5},{5,9},{9,13},{2,6},{6,10},{10,14},{3,7},{... | collective-permute-start | bytes 2211848 | tf_op jit(solution)/shard_map/ppermute | solution.py:24
  254.9 20.5 %copy-start.5 = (f32[4,62,32,1]{1,0,2,3:T(4,128)S(1)}, f32[4,62,32,1]{1,0,2,3:T(4,128)}, u32[]{:S(2)}) copy-start(f32[4,62,32,1]{1,0,2,3:T(4,128)} %copy-done.4) | copy-start | bytes 95236
  254.9 20.3 %collective-permute-start.15 = (f32[4,24,15,128]{3,1,2,0:T(8,128)S(1)}, f32[4,24,15,128]{3,1,2,0:T(8,128)S(1)}, u32[]{:S(2)}, u32[]{:S(2)}) collective-permute-start(f32[4,24,15,128]{3,1,2,0:T(8,128)S(1)} %get-tuple-element.61), channel_id=1, source_target_pairs={{4,0},{8,4},{12,8},{5,1},{9,5},{13,9},{6,2},{10,6},{14,10},{7,3},{... | collective-permute-start | bytes 2211848 | tf_op jit(solution)/shard_map/ppermute | solution.py:27
  282.8 44.8 %collective-permute-start.16 = (f32[4,24,32,15]{2,1,3,0:T(8,128)}, f32[4,24,32,15]{2,1,3,0:T(8,128)}, u32[]{:S(2)}, u32[]{:S(2)}) collective-permute-start(f32[4,24,32,15]{2,1,3,0:T(8,128)} %copy.55), channel_id=1, source_target_pairs={{0,1},{1,2},{2,3},{4,5},{5,6},{6,7},{8,9},{9,10},{10,11},{12,13},{... | collective-permute-start | bytes 552968 | tf_op jit(solution)/shard_map/ppermute | solution.py:24
  299.0 36.9 %collective-permute-start.17 = (f32[4,24,32,15]{2,1,3,0:T(8,128)}, f32[4,24,32,15]{2,1,3,0:T(8,128)}, u32[]{:S(2)}, u32[]{:S(2)}) collective-permute-start(f32[4,24,32,15]{2,1,3,0:T(8,128)} %copy.56), channel_id=1, source_target_pairs={{1,0},{2,1},{3,2},{5,4},{6,5},{7,6},{9,8},{10,9},{11,10},{13,12},{... | collective-permute-start | bytes 552968 | tf_op jit(solution)/shard_map/ppermute | solution.py:27
  338.8 7.0 %copy-start.13 = (f32[4]{0:T(128)S(1)}, f32[4]{0:T(128)}, u32[]{:S(2)}) copy-start(f32[4]{0:T(128)} %get-tuple-element.5) | copy-start | bytes 52
  381.2 15.4 %collective-permute-start.18 = (f32[4,15,32,128]{3,2,1,0:T(8,128)S(1)}, f32[4,15,32,128]{3,2,1,0:T(8,128)S(1)}, u32[]{:S(2)}, u32[]{:S(2)}) collective-permute-start(f32[4,15,32,128]{3,2,1,0:T(8,128)S(1)} %get-tuple-element.56), channel_id=1, source_target_pairs={{0,16},{16,32},{32,48},{48,64},{64,80},{80,96},{96,112},{112,128},... | collective-permute-start | bytes 2949128 | tf_op jit(solution)/shard_map/ppermute | solution.py:24
  383.2 15.8 %copy-start.7 = (f32[4,54,24,1]{1,0,2,3:T(4,128)S(1)}, f32[4,54,24,1]{1,0,2,3:T(4,128)}, u32[]{:S(2)}) copy-start(f32[4,54,24,1]{1,0,2,3:T(4,128)} %copy-done.6) | copy-start | bytes 62212
  383.2 15.4 %collective-permute-start.19 = (f32[4,15,32,128]{3,2,1,0:T(8,128)S(1)}, f32[4,15,32,128]{3,2,1,0:T(8,128)S(1)}, u32[]{:S(2)}, u32[]{:S(2)}) collective-permute-start(f32[4,15,32,128]{3,2,1,0:T(8,128)S(1)} %get-tuple-element.57), channel_id=1, source_target_pairs={{16,0},{32,16},{48,32},{64,48},{80,64},{96,80},{112,96},{128,112},... | collective-permute-start | bytes 2949128 | tf_op jit(solution)/shard_map/ppermute | solution.py:27
  403.0 18.7 %collective-permute-start.20 = (f32[4,24,15,128]{3,1,2,0:T(8,128)S(1)}, f32[4,24,15,128]{3,1,2,0:T(8,128)S(1)}, u32[]{:S(2)}, u32[]{:S(2)}) collective-permute-start(f32[4,24,15,128]{3,1,2,0:T(8,128)S(1)} %get-tuple-element.54), channel_id=1, source_target_pairs={{0,4},{4,8},{8,12},{1,5},{5,9},{9,13},{2,6},{6,10},{10,14},{3,7},{... | collective-permute-start | bytes 2211848 | tf_op jit(solution)/shard_map/ppermute | solution.py:24
  406.1 20.6 %copy-start.3 = (f32[4,62,32,1]{1,0,2,3:T(4,128)S(1)}, f32[4,62,32,1]{1,0,2,3:T(4,128)}, u32[]{:S(2)}) copy-start(f32[4,62,32,1]{1,0,2,3:T(4,128)} %copy-done.2) | copy-start | bytes 95236
  406.1 20.4 %collective-permute-start.21 = (f32[4,24,15,128]{3,1,2,0:T(8,128)S(1)}, f32[4,24,15,128]{3,1,2,0:T(8,128)S(1)}, u32[]{:S(2)}, u32[]{:S(2)}) collective-permute-start(f32[4,24,15,128]{3,1,2,0:T(8,128)S(1)} %get-tuple-element.55), channel_id=1, source_target_pairs={{4,0},{8,4},{12,8},{5,1},{9,5},{13,9},{6,2},{10,6},{14,10},{7,3},{... | collective-permute-start | bytes 2211848 | tf_op jit(solution)/shard_map/ppermute | solution.py:27
  433.7 36.1 %collective-permute-start.22 = (f32[4,24,32,15]{2,1,3,0:T(8,128)}, f32[4,24,32,15]{2,1,3,0:T(8,128)}, u32[]{:S(2)}, u32[]{:S(2)}) collective-permute-start(f32[4,24,32,15]{2,1,3,0:T(8,128)} %copy.64), channel_id=1, source_target_pairs={{0,1},{1,2},{2,3},{4,5},{5,6},{6,7},{8,9},{9,10},{10,11},{12,13},{... | collective-permute-start | bytes 552968 | tf_op jit(solution)/shard_map/ppermute | solution.py:24
  440.3 37.5 %collective-permute-start.23 = (f32[4,24,32,15]{2,1,3,0:T(8,128)}, f32[4,24,32,15]{2,1,3,0:T(8,128)}, u32[]{:S(2)}, u32[]{:S(2)}) collective-permute-start(f32[4,24,32,15]{2,1,3,0:T(8,128)} %copy.65), channel_id=1, source_target_pairs={{1,0},{2,1},{3,2},{5,4},{6,5},{7,6},{9,8},{10,9},{11,10},{13,12},{... | collective-permute-start | bytes 552968 | tf_op jit(solution)/shard_map/ppermute | solution.py:27
where the time goes:
time: 497 us; the launch traced here: 487 us
  waiting for transfers between devices  222 us (45%)
  blocking collectives  75.2 us (15%)
  starting transfers between devices  72.2 us (15%)
  local copies, waits for them, and re-layouts  56.4 us (11%)
  matrix products  48.9 us (10%)
  other arithmetic  10.6 us (2%)
    ppermute x12, waiting for transfers between devices, extended(): lax.ppermute(lax.slice_in_dim(block, block.shape[dim] - width, None, axis...  184 us
    psum x10, blocking collectives, one_axis_at_a_time(): return functools.reduce(lax.psum, axes, shard)  75.2 us
    ppermute x12, starting transfers between devices, extended(): lax.ppermute(lax.slice_in_dim(block, block.shape[dim] - width, None, axis...  46.3 us
    dot_general x12, matrix products, product(): return jnp.einsum(form, left, right, precision=lax.Precision.HIGHEST)  45.4 us
    ppermute x12, waiting for transfers between devices, extended(): lax.ppermute(lax.slice_in_dim(block, 0, width, axis=dim), axis, backward)  38.2 us
    ppermute x12, starting transfers between devices, extended(): lax.ppermute(lax.slice_in_dim(block, 0, width, axis=dim), axis, backward)  25.9 us
    slice x16, local copies, waits for them, and re-layouts, extended(): lax.slice_in_dim(block, block.shape[dim] - width, None, axis=dim)  23.2 us
    ppermute x4, local copies, waits for them, and re-layouts, extended(): lax.ppermute(lax.slice_in_dim(block, 0, width, axis=dim), axis, backward)  11.7 us
  transfers between devices with their start and end apart: 24, of which 22 were waited for; matrix products, arithmetic and copies ran while one was open for 5% of the time, Pallas kernels for 0%

commit v1 on v0

v1 whole, which is shorter than its diff:
```python
import functools

import jax
import jax.numpy as jnp
from jax import lax
from jax.experimental import pallas as pl
from jax.experimental.pallas import tpu as pltpu
from jax.sharding import Mesh
from jax.sharding import PartitionSpec as P

TAPS = 31
REACH = 15
ITERS = 2
VIEWS = 4
X, Y, Z = 24, 32, 128
YE = 64
F32 = jnp.float32
BF16 = jnp.bfloat16
GX = ("gx_0", "gx_1", "gx_2")
AXES = {"gx": GX, "gy": "gy", "gz": "gz"}
SUM_STEPS = (("gx_2", 1), ("gx_1", 1), ("gx_1", 2), ("gy", 1), ("gy", 2), ("gx_0", 1), ("gz", 1), ("gz", 2))


def parity(name):
    if name == "gx":
        return lax.axis_index("gx_2")
    return lax.rem(lax.axis_index(name), 2)


def position(name):
    if name == "gx":
        return (lax.axis_index("gx_0") * 4 + lax.axis_index("gx_1")) * 2 + lax.axis_index("gx_2")
    return lax.axis_index(name)


def lanes(shape):
    return lax.broadcasted_iota(jnp.int32, shape, len(shape) - 1)


def split(value):
    high = value.astype(BF16)
    low = (value - high.astype(F32)).astype(BF16)
    return high, low


def left_exact(matrix, data):
    high, low = split(data)
    return jnp.dot(matrix, high, preferred_element_type=F32) + jnp.dot(matrix, low, preferred_element_type=F32)


def right_exact(data, matrix):
    rows = data.shape[0]
    both = jnp.dot(jnp.concatenate(split(data), axis=0), matrix, preferred_element_type=F32)
    return both[:rows] + both[rows:]


def extended_offset(index, size, width, odd):
    low_first = index < size + width
    local = jnp.where(low_first, index - size, index - size - width)
    upper = low_first == (odd == 0)
    outside = jnp.where(upper, size + local, local - width)
    return jnp.where(index < size, index, outside)


def taps_matrix(taps_ref, view, axis, source, target):
    tap = source - target + REACH
    out = jnp.zeros(tap.shape, F32)
    for t in range(TAPS):
        out = jnp.where(tap == t, taps_ref[view, axis, t].astype(F32) / 256.0, out)
    return out


def select_matrix(rows, columns, match):
    r = lax.broadcasted_iota(jnp.int32, (rows, columns), 0)
    c = lax.broadcasted_iota(jnp.int32, (rows, columns), 1)
    return match(r, c)


def one_hot(rows, columns, match):
    return jnp.where(select_matrix(rows, columns, match), 1.0, 0.0).astype(BF16)


def setup_kernel(taps_ref, fz, fy, fx, bz, by, bx, ax, ayz):
    odd_x, odd_y, odd_z = parity("gx"), parity("gy"), parity("gz")
    XE = X + 2 * REACH
    for v in range(VIEWS):
        src = extended_offset(lax.broadcasted_iota(jnp.int32, (256, Z), 0), Z, 16, odd_z)
        raw = lax.broadcasted_iota(jnp.int32, (256, Z), 0)
        tgt = lax.broadcasted_iota(jnp.int32, (256, Z), 1)
        src = jnp.where(raw < Z + 32, src, -1000)
        fz[:, v * Z : (v + 1) * Z] = taps_matrix(taps_ref, v, 2, src, tgt).astype(BF16)
        raw = lax.broadcasted_iota(jnp.int32, (Z, 256), 1)
        src = extended_offset(raw, Z, 16, odd_z)
        src = jnp.where(raw < Z + 32, src, -1000)
        tgt = lax.broadcasted_iota(jnp.int32, (Z, 256), 0)
        bz[v * Z : (v + 1) * Z, :] = taps_matrix(taps_ref, v, 2, src, tgt).astype(BF16)
        tgt = lax.broadcasted_iota(jnp.int32, (Y, YE), 0)
        src = extended_offset(lax.broadcasted_iota(jnp.int32, (Y, YE), 1), Y, 16, odd_y)
        base = taps_matrix(taps_ref, v, 1, src, tgt).astype(BF16)
        spread = jnp.dot(one_hot(4 * Y, Y, lambda r, c: lax.rem(r, Y) == c), base, preferred_element_type=F32).astype(BF16)
        spread = jnp.dot(spread, one_hot(YE, 4 * YE, lambda r, c: lax.rem(c, YE) == r), preferred_element_type=F32)
        mask = select_matrix(4 * Y, 4 * YE, lambda r, c: r // Y == c // YE)
        spread = jnp.where(mask, spread, 0.0)
        fy[v] = spread.astype(BF16)
        by[v] = spread.T.astype(BF16)
        tgt = lax.broadcasted_iota(jnp.int32, (X, XE), 0)
        src = extended_offset(lax.broadcasted_iota(jnp.int32, (X, XE), 1), X, REACH, odd_x)
        base = taps_matrix(taps_ref, v, 0, src, tgt).astype(BF16)
        spread = jnp.dot(one_hot(X * 8, X, lambda r, c: r // 8 == c), base, preferred_element_type=F32).astype(BF16)
        spread = jnp.dot(spread, one_hot(XE, XE * 8, lambda r, c: c // 8 == r), preferred_element_type=F32)
        mask = select_matrix(X * 8, XE * 8, lambda r, c: lax.rem(r, 8) == lax.rem(c, 8))
        spread = jnp.where(mask, spread, 0.0)
        fx[v] = spread.astype(BF16)
        by_t = jnp.concatenate([spread, jnp.zeros((X * 8, 512 - XE * 8), F32)], axis=1).T
        bx[v] = by_t[: XE * 8].astype(BF16)
        def reachable(axis, name, size, count, iota):
            where_global = position(name) * size + iota
            out = jnp.zeros(iota.shape, F32)
            for t in range(TAPS):
                at = where_global - t + REACH
                inside = (at >= 0) & (at < count * size)
                out = out + jnp.where(inside, taps_ref[v, axis, t].astype(F32) / 256.0, 0.0)
            return out
        ax[v] = reachable(0, "gx", X, 16, lax.broadcasted_iota(jnp.int32, (X, Z), 0))
        ayz[v] = reachable(1, "gy", Y, 4, lax.broadcasted_iota(jnp.int32, (Y, Z), 0)) * reachable(
            2, "gz", Z, 4, lax.broadcasted_iota(jnp.int32, (Y, Z), 1)
        )


def pack_z(load, z_a, z_b):
    group = lanes((3 * Y, Z)) // 16
    up = jnp.zeros((3 * Y, Z), F32)
    down = jnp.zeros((3 * Y, Z), F32)
    for g in range(8):
        part = load(g)
        up = jnp.where(group == g, pltpu.roll(part, (16 * g + 16) % Z, 1) if g != 7 else part, up)
        down = jnp.where(group == g, pltpu.roll(part, 16 * g, 1) if g else part, down)
    odd = parity("gz")
    z_a[...] = jnp.where(odd == 0, up, down)
    z_b[...] = jnp.where(odd == 0, down, up)


def blurred_totals(load, ax, ayz):
    lane = lanes((8, Z))
    row = lax.broadcasted_iota(jnp.int32, (8, Z), 0)
    out = jnp.zeros((8, Z), F32)
    for v in range(VIEWS):
        acc = jnp.zeros((Y, Z), F32)
        for i in range(X):
            acc = acc + load(i) * ax[v, i : i + 1, :]
        total = jnp.sum(acc * ayz[v])
        out = jnp.where((lane == 8 + v) & (row == 0), total, out)
    return out


def first_kernel(est, z_a, z_b):
    pack_z(lambda g: est[3 * g : 3 * g + 3].reshape(3 * Y, Z), z_a, z_b)


def sums_kernel(est, views, ax, ayz, row_ref):
    lane = lanes((8, Z))
    row = lax.broadcasted_iota(jnp.int32, (8, Z), 0)
    out = blurred_totals(lambda i: est[i], ax, ayz)
    for v in range(VIEWS):
        total = jnp.zeros((Y, Z), F32)
        square = jnp.zeros((Y, Z), F32)
        for i in range(X):
            image = views[v, i]
            total = total + image
            square = square + image * image
        out = jnp.where((lane == v) & (row == 0), jnp.sum(total), out)
        out = jnp.where((lane == 4 + v) & (row == 0), jnp.sum(square), out)
    row_ref[...] = out


def pack_y_kernel(est, z_a, z_b, y_a, y_b):
    odd = parity("gy")
    start_a = pl.multiple_of((1 - odd) * 16, 16)
    start_b = pl.multiple_of(odd * 16, 16)
    for start, out in ((start_a, y_a), (start_b, y_b)):
        out[0:X] = est[:, pl.ds(start, 16), :]
        out[X : X + 3] = z_a[:, pl.ds(start, 16), :]
        out[X + 3 : X + 6] = z_b[:, pl.ds(start, 16), :]


def pack_x_kernel(est, z_a, z_b, y_a, y_b, own, x_a, x_b):
    own[0:X, 0:Y] = est[...]
    own[X : X + 3, 0:Y] = z_a[...]
    own[X + 3 : X + 6, 0:Y] = z_b[...]
    own[:, Y : Y + 16] = y_a[...]
    own[:, Y + 16 : YE] = y_b[...]
    odd = parity("gx")
    for flag, out in ((odd, x_a), (1 - odd, x_b)):
        out[0:REACH] = own[pl.ds((1 - flag) * 9, REACH)]
        for i in range(6):
            full = own[X + i]
            out[REACH + i] = jnp.where(flag == 0, pltpu.roll(full, Z - 48, 1), full)


def forward_group(src, first_z, plane, fz, fy, store):
    mains, sides = [], []
    lane = lanes((YE, Z))
    for k in range(4):
        p = plane + k
        g = p // 3
        i = p - 3 * g
        mains.append(src[p])
        a = pltpu.roll(src[first_z + i], lax.rem(Z - 16 * g, Z), 1)
        b = pltpu.roll(src[first_z + 3 + i], lax.rem(Z + 16 - 16 * g, Z), 1)
        sides.append(jnp.where(lane < 16, a, b))
    data = jnp.concatenate([jnp.concatenate(mains, 0), jnp.concatenate(sides, 0)], axis=1)
    wide = right_exact(data, fz[...])
    for v in range(VIEWS):
        out = left_exact(fy[v], wide[:, v * Z : (v + 1) * Z])
        store(v, out.reshape(4, Y, Z))


def forward_own_kernel(own, fz, fy, out):
    def step(j, carry):
        plane = j * 4

        def store(v, value):
            out[v, pl.ds(plane, 4)] = value

        forward_group(own, X, plane, fz, fy, store)
        return carry

    lax.fori_loop(0, 6, step, 0)


def forward_kernel(x_a, x_b, mid, fz, fy, fx, out, halo):
    for base, src in ((0, x_a), (REACH, x_b)):
        def step(j, carry, base=base, src=src):
            plane = jnp.minimum(j * 4, REACH - 4)

            def store(v, value):
                halo[v, pl.ds(base + plane, 4)] = value

            forward_group(src, REACH, plane, fz, fy, store)
            return carry

        lax.fori_loop(0, 4, step, 0)
    for v in range(VIEWS):
        for pair in range(2):
            columns = []
            for tile in (2 * pair, 2 * pair + 1):
                rows = pl.ds(tile * 8, 8)
                columns.append(
                    jnp.concatenate(
                        [mid[v, :, rows].reshape(X * 8, Z), halo[v, :, rows].reshape(2 * REACH * 8, Z)], axis=0
                    )
                )
            got = left_exact(fx[v], jnp.concatenate(columns, axis=1))
            for k, tile in enumerate((2 * pair, 2 * pair + 1)):
                out[v, :, tile * 8 : tile * 8 + 8] = got[:, k * Z : (k + 1) * Z].reshape(X, 8, Z)


def pick(row, lane, index):
    return jnp.sum(jnp.where(lane == index, row, 0.0), axis=1, keepdims=True)


def backward_group(load, plane, bz, by, store):
    parts = [left_exact(by[v], load(v, plane).reshape(4 * Y, Z)) for v in range(VIEWS)]
    wide = right_exact(jnp.concatenate(parts, axis=1), bz[...])
    store(wide)


def store_extended(dst, first_z, plane, wide):
    group = lanes((YE, Z)) // 16
    for k in range(4):
        p = plane + k
        g = p // 3
        i = p - 3 * g
        rows = wide[k * YE : (k + 1) * YE]
        dst[p] = rows[:, :Z]
        side = rows[:, Z:]
        a = pltpu.roll(side, lax.rem(16 * g + Z, Z), 1)
        b = pltpu.roll(side, lax.rem(16 * g + Z - 16, Z), 1)
        dst[first_z + i] = jnp.where(group == g, a, dst[first_z + i])
        dst[first_z + 3 + i] = jnp.where(group == g, b, dst[first_z + 3 + i])


def backward_kernel(sums, weights, norm, blurred, views, bz, by, bx, x_a, x_b, mid, misfit, halo):
    lane = lanes((1, Z))
    row = sums[0:1, :]
    out_lane = lanes((8, Z))
    out_row = lax.broadcasted_iota(jnp.int32, (8, Z), 0)
    misfits = jnp.zeros((8, Z), F32)
    for v in range(VIEWS):
        flux = pick(row, lane, v) / pick(row, lane, 8 + v)
        scale = weights[v].astype(F32) / norm[0]
        missed = jnp.zeros((X * 8, 2 * Z), F32)
        for pair in range(2):
            tiles = (2 * pair, 2 * pair + 1)
            b = jnp.concatenate([blurred[v, :, t * 8 : t * 8 + 8].reshape(X * 8, Z) for t in tiles], axis=1)
            image = jnp.concatenate([views[v, :, t * 8 : t * 8 + 8].reshape(X * 8, Z) for t in tiles], axis=1)
            scaled = flux * b
            gap = image - scaled
            missed = missed + gap * gap
            got = left_exact(bx[v], (image / scaled) * scale)
            for k, t in enumerate(tiles):
                piece = got[:, k * Z : (k + 1) * Z]
                mid[v, :, t * 8 : t * 8 + 8] = piece[: X * 8].reshape(X, 8, Z)
                halo[v, :, t * 8 : t * 8 + 8] = piece[X * 8 :].reshape(2 * REACH, 8, Z)
        misfits = jnp.where((out_lane == 12 + v) & (out_row == 0), jnp.sum(missed), misfits)
    misfit[...] = misfits
    for base, dst in ((0, x_a), (REACH, x_b)):
        dst[REACH : REACH + 6] = jnp.zeros((6, YE, Z), F32)

        def step(j, carry, base=base, dst=dst):
            plane = jnp.minimum(j * 4, REACH - 4)
            backward_group(
                lambda v, p: halo[v, pl.ds(base + p, 4)],
                plane, bz, by, lambda wide: store_extended(dst, REACH, plane, wide),
            )
            return carry

        lax.fori_loop(0, 4, step, 0)


def backward_own_kernel(mid, bz, by, own):
    own[X : X + 6] = jnp.zeros((6, YE, Z), F32)

    def step(j, carry):
        plane = j * 4
        backward_group(
            lambda v, p: mid[v, pl.ds(p, 4)], plane, bz, by, lambda wide: store_extended(own, X, plane, wide)
        )
        return carry

    lax.fori_loop(0, 6, step, 0)


def add_x_kernel(own, x_a, x_b, kept, y_a, y_b, total):
    total[...] = own[...]
    odd = parity("gx")
    valid = lanes((YE, Z)) < 80
    for flag, src in ((odd, x_a), (1 - odd, x_b)):
        spot = pl.ds((1 - flag) * 9, REACH)
        total[spot] = total[spot] + src[0:REACH]
        for i in range(6):
            side = jnp.where(valid, src[REACH + i], 0.0)
            total[X + i] = total[X + i] + jnp.where(flag == 0, pltpu.roll(side, 48, 1), side)
    kept[...] = total[:, 0:Y]
    y_a[...] = total[:, Y : Y + 16]
    y_b[...] = total[:, Y + 16 : YE]


def add_y_kernel(kept, y_a, y_b, main, z_a, z_b, total):
    total[...] = kept[...]
    odd = parity("gy")
    for start, src in (((1 - odd) * 16, y_a), (odd * 16, y_b)):
        spot = pl.ds(pl.multiple_of(start, 16), 16)
        total[:, spot] = total[:, spot] + src[...]
    main[...] = total[0:X]
    z_a[...] = total[X : X + 3]
    z_b[...] = total[X + 3 : X + 6]


def corrected(main, z_a, z_b, est, g):
    odd = parity("gz")
    lane = lanes((3 * Y, Z))
    a = z_a[...].reshape(3 * Y, Z)
    b = z_b[...].reshape(3 * Y, Z)
    up = jnp.where(odd == 0, a, b)
    down = jnp.where(odd == 0, b, a)
    up = pltpu.roll(up, (112 - 16 * g) % Z, 1) if g != 7 else up
    down = pltpu.roll(down, (Z - 16 * g) % Z, 1) if g else down
    total = main[3 * g : 3 * g + 3].reshape(3 * Y, Z)
    total = total + jnp.where(lane >= 112, up, 0.0) + jnp.where(lane < 16, down, 0.0)
    return est[3 * g : 3 * g + 3].reshape(3 * Y, Z) * total


def update_kernel(main, z_a, z_b, est, ax, ayz, carry, out, out_a, out_b, row_ref):
    for g in range(8):
        out[3 * g : 3 * g + 3] = corrected(main, z_a, z_b, est, g).reshape(3, Y, Z)
    pack_z(lambda g: out[3 * g : 3 * g + 3].reshape(3 * Y, Z), out_a, out_b)
    row_ref[...] = blurred_totals(lambda i: out[i], ax, ayz) + carry[...]


def finish_kernel(main, z_a, z_b, est, out):
    for g in range(8):
        out[3 * g : 3 * g + 3] = corrected(main, z_a, z_b, est, g).reshape(3, Y, Z)


VM = pl.BlockSpec(memory_space=pltpu.VMEM)
SM = pl.BlockSpec(memory_space=pltpu.SMEM)


def call(kernel, outs, operands, specs=None, scratch=(), limit=16, flops=0):
    shapes = [jax.ShapeDtypeStruct(shape, dtype) for shape, dtype in outs]
    return pl.pallas_call(
        kernel,
        out_shape=shapes,
        in_specs=specs or [VM] * len(operands),
        out_specs=[VM] * len(shapes),
        scratch_shapes=[pltpu.VMEM(shape, dtype) for shape, dtype in scratch],
        compiler_params=pltpu.CompilerParams(vmem_limit_bytes=limit << 20),
        cost_estimate=pl.CostEstimate(flops=max(flops, 1000), bytes_accessed=1000, transcendentals=0),
        name=kernel.__name__,
    )(*operands)


def swap(a, b, axis):
    names = AXES[axis]
    count = lax.axis_size(names)
    first = [(i, i ^ 1) for i in range(count)]
    second = [(i, i + 1) for i in range(1, count - 1, 2)] + [(i + 1, i) for i in range(1, count - 1, 2)]
    return lax.ppermute(a, names, first), lax.ppermute(b, names, second)


def all_sum(row):
    for axis, bit in SUM_STEPS:
        count = lax.axis_size(axis)
        row = row + lax.ppermute(row, axis, [(i, i ^ bit) for i in range(count)])
    return row


ZS = ((3 * Y, Z), F32)
Z3 = ((3, Y, Z), F32)
YS = ((X + 6, 16, Z), F32)
XS = ((REACH + 6, YE, Z), F32)
OWN = ((X + 6, YE, Z), F32)
CUBE = ((X, Y, Z), F32)
FOUR = ((VIEWS, X, Y, Z), F32)
ROW = ((8, Z), F32)
GF = 1 << 30


def local(estimate, view_images, psf_taps, view_weights):
    XE8 = (X + 2 * REACH) * 8
    kernels = psf_taps.astype(F32) / 256.0
    tap_sums = jnp.sum(kernels, axis=2)
    norm = jnp.sum(view_weights.astype(F32) * jnp.prod(tap_sums, axis=1)).reshape(1)
    z_a, z_b = call(first_kernel, [ZS, ZS], [estimate])
    fz, fy, fx, bz, by, bx, ax, ayz = call(
        setup_kernel,
        [
            ((256, VIEWS * Z), BF16), ((VIEWS, 4 * Y, 4 * YE), BF16), ((VIEWS, X * 8, XE8), BF16),
            ((VIEWS * Z, 256), BF16), ((VIEWS, 4 * YE, 4 * Y), BF16), ((VIEWS, XE8, X * 8), BF16),
            ((VIEWS, X, Z), F32), ((VIEWS, Y, Z), F32),
        ],
        [psf_taps], specs=[SM], limit=24, flops=4 * GF,
    )
    (row,) = call(sums_kernel, [ROW], [estimate, view_images, ax, ayz], flops=GF)
    data = None
    misfits = []
    for iteration in range(ITERS):
        z_a, z_b = swap(z_a, z_b, "gz")
        z_a, z_b = z_a.reshape(3, Y, Z), z_b.reshape(3, Y, Z)
        sums = all_sum(row)
        y_a, y_b = call(pack_y_kernel, [YS, YS], [estimate, z_a, z_b])
        y_a, y_b = swap(y_a, y_b, "gy")
        own, x_a, x_b = call(pack_x_kernel, [OWN, XS, XS], [estimate, z_a, z_b, y_a, y_b])
        x_a, x_b = swap(x_a, x_b, "gx")
        (mid,) = call(forward_own_kernel, [FOUR], [own, fz, fy], flops=3 * GF)
        (blurred,) = call(
            forward_kernel, [FOUR], [x_a, x_b, mid, fz, fy, fx],
            scratch=[((VIEWS, 2 * REACH, Y, Z), F32)], limit=24, flops=4 * GF,
        )
        if iteration == 0:
            data = sums
        else:
            lane = lax.broadcasted_iota(jnp.int32, (8, Z), 1)
            data = jnp.where(lane < 8, data, sums)
        x_a, x_b, mid, missed = call(
            backward_kernel, [XS, XS, FOUR, ROW], [data, view_weights, norm, blurred, view_images, bz, by, bx],
            specs=[VM, SM, SM] + [VM] * 5,
            scratch=[((VIEWS, 2 * REACH, Y, Z), F32)], limit=24, flops=4 * GF,
        )
        x_a, x_b = swap(x_a, x_b, "gx")
        (own,) = call(backward_own_kernel, [OWN], [mid, bz, by], flops=3 * GF)
        kept, y_a, y_b = call(
            add_x_kernel, [((X + 6, Y, Z), F32), YS, YS], [own, x_a, x_b], scratch=[OWN],
        )
        y_a, y_b = swap(y_a, y_b, "gy")
        main, z_a, z_b = call(add_y_kernel, [CUBE, Z3, Z3], [kept, y_a, y_b], scratch=[((X + 6, Y, Z), F32)])
        z_a, z_b = swap(z_a, z_b, "gz")
        if iteration + 1 < ITERS:
            estimate, z_a, z_b, row = call(
                update_kernel, [CUBE, ZS, ZS, ROW], [main, z_a, z_b, estimate, ax, ayz, missed]
            )
        else:
            last = all_sum(missed)
            (estimate,) = call(finish_kernel, [CUBE], [main, z_a, z_b, estimate])
            misfits = [data[0, 12:16] / data[0, 4:8], last[0, 12:16] / data[0, 4:8]]
    return (estimate, jnp.stack(misfits))


def solution(mesh):
    torus = Mesh(
        mesh.devices.reshape(2, 4, 2, mesh.shape["gy"], mesh.shape["gz"]),
        ("gx_0", "gx_1", "gx_2", "gy", "gz"),
    )
    in_specs = (P(GX, "gy", "gz"), P(None, GX, "gy", "gz"), P(), P())
    out_specs = (P(GX, "gy", "gz"), P())
    return jax.shard_map(local, mesh=torus, in_specs=in_specs, out_specs=out_specs, check_vma=False)
```

time: 497 us -> 268 us (0.54)
  the two profiles are of different devices: /device:TPU:34 before, /device:TPU:168 now
where the time goes in v1:
time: 268 us; the launch traced here: 264 us
  waiting for transfers between devices  142 us (53%)
  starting transfers between devices  61.9 us (23%)
  Pallas kernels  52.8 us (20%)
  local copies, waits for them, and re-layouts  4.55 us (2%)
    ppermute x24, waiting for transfers between devices, all_sum(): row = row + lax.ppermute(row, axis, [(i, i ^ bit) for i in range(count)])  99.1 us
    pallas_call x21, Pallas kernels, call(): pl.pallas_call(kernel, out_shape=shapes, in_specs=specs or [VM] * len(ope...  52.8 us
    ppermute x24, waiting for transfers between devices, swap(): return (lax.ppermute(a, names, first), lax.ppermute(b, names, second))  42.7 us
    ppermute x24, starting transfers between devices, swap(): return (lax.ppermute(a, names, first), lax.ppermute(b, names, second))  41.5 us
    ppermute x24, starting transfers between devices, all_sum(): row = row + lax.ppermute(row, axis, [(i, i ^ bit) for i in range(count)])  20.5 us
  transfers between devices with their start and end apart: 48, of which 38 were waited for; matrix products, arithmetic and copies ran while one was open for 1% of the time, Pallas kernels for 8%

profile of v1, /device:TPU:168, one launch (start us, length us, event | category | flops | bytes accessed | tf_op | source)
XLA Modules:
  0.0 263.8 jit_solution(1973987166326909367)
XLA Ops:
  1.9 1.6 collective-permute-start.8
  3.4 1.9 collective-permute-start.9
  5.4 1.7 collective-permute-done.8
  7.0 5.0 %collective-permute-done.9 = f32[96,128]{1,0:T(8,128)S(1)} collective-permute-done((f32[96,128]{1,0:T(8,128)S(1)}, f32[96,128]{1,0:T(8,128)S(1)}, u32[]{:S(2)}, u32[]{:S(2)}) %collective-permute-start.9) | collective-permute-done | bytes 49184 | tf_op jit(solution)/shard_map/ppermute | solution.py:409
  12.6 4.3 %collective-permute-start.11 = (f32[30,16,128]{2,1,0:T(8,128)S(1)}, f32[30,16,128]{2,1,0:T(8,128)S(1)}, u32[]{:S(2)}, u32[]{:S(2)}) collective-permute-start(f32[30,16,128]{2,1,0:T(8,128)S(1)} %get-tuple-element.51), channel_id=1, source_target_pairs={{4,8},{8,4},{5,9},{9,5},{6,10},{10,6},{7,11},{11,7},{20,24},{24,20... | collective-permute-start | bytes 737288 | tf_op jit(solution)/shard_map/ppermute | solution.py:409
  18.4 2.7 %collective-permute-done.11.y_b = f32[30,16,128]{2,1,0:T(8,128)S(1)} collective-permute-done((f32[30,16,128]{2,1,0:T(8,128)S(1)}, f32[30,16,128]{2,1,0:T(8,128)S(1)}, u32[]{:S(2)}, u32[]{:S(2)}) %collective-permute-start.11) | collective-permute-done | bytes 245792 | tf_op jit(solution)/shard_map/ppermute | solution.py:409
  21.1 1.3 pack_x_kernel.2
  22.4 5.0 %collective-permute-start.13 = (f32[21,64,128]{2,1,0:T(8,128)}, f32[21,64,128]{2,1,0:T(8,128)}, u32[]{:S(2)}, u32[]{:S(2)}) collective-permute-start(f32[21,64,128]{2,1,0:T(8,128)} %get-tuple-element.53), channel_id=1, source_target_pairs={{16,32},{48,64},{80,96},{112,128},{144,160},{176,192},{208,224},{3... | collective-permute-start | bytes 2064392 | tf_op jit(solution)/shard_map/ppermute | solution.py:409
  27.4 4.7 %setup_kernel.1 = (bf16[256,512]{1,0:T(8,128)(2,1)S(1)}, bf16[4,128,256]{2,1,0:T(8,128)(2,1)S(1)}, bf16[4,192,432]{2,1,0:T(8,128)(2,1)S(1)}, bf16[512,256]{1,0:T...) custom-call(s32[4,3,31]{2,1,0:T(4,128)S(1)} %copy.7.taps_ref), custom_call_target="tpu_custom_call" | custom-call | flops 4294967296 | bytes 1000 | tf_op jit(solution)/shard_map/setup_kernel/pallas_call | solution.py:392
  33.5 1.2 collective-permute-done
  34.7 3.6 %collective-permute-done.1 = f32[8,128]{1,0:T(8,128)S(1)} collective-permute-done((f32[8,128]{1,0:T(8,128)S(1)}, f32[8,128]{1,0:T(8,128)S(1)}, u32[]{:S(2)}, u32[]{:S(2)}) %collective-permute-start.1) | collective-permute-done | bytes 4128 | tf_op jit(solution)/shard_map/ppermute | solution.py:415
  39.4 4.0 %collective-permute-done.2 = f32[8,128]{1,0:T(8,128)S(1)} collective-permute-done((f32[8,128]{1,0:T(8,128)S(1)}, f32[8,128]{1,0:T(8,128)S(1)}, u32[]{:S(2)}, u32[]{:S(2)}) %collective-permute-start.2) | collective-permute-done | bytes 4128 | tf_op jit(solution)/shard_map/ppermute | solution.py:415
  43.4 3.6 %collective-permute-done.3 = f32[8,128]{1,0:T(8,128)S(1)} collective-permute-done((f32[8,128]{1,0:T(8,128)S(1)}, f32[8,128]{1,0:T(8,128)S(1)}, u32[]{:S(2)}, u32[]{:S(2)}) %collective-permute-start.3) | collective-permute-done | bytes 4128 | tf_op jit(solution)/shard_map/ppermute | solution.py:415
  47.0 1.3 collective-permute-start.4
  48.4 3.8 %collective-permute-done.4 = f32[8,128]{1,0:T(8,128)S(1)} collective-permute-done((f32[8,128]{1,0:T(8,128)S(1)}, f32[8,128]{1,0:T(8,128)S(1)}, u32[]{:S(2)}, u32[]{:S(2)}) %collective-permute-start.4) | collective-permute-done | bytes 4128 | tf_op jit(solution)/shard_map/ppermute | solution.py:415
  52.2 3.6 %collective-permute-done.5 = f32[8,128]{1,0:T(8,128)S(1)} collective-permute-done((f32[8,128]{1,0:T(8,128)S(1)}, f32[8,128]{1,0:T(8,128)S(1)}, u32[]{:S(2)}, u32[]{:S(2)}) %collective-permute-start.5) | collective-permute-done | bytes 4128 | tf_op jit(solution)/shard_map/ppermute | solution.py:415
  55.9 4.4 %collective-permute-done.6 = f32[8,128]{1,0:T(8,128)S(1)} collective-permute-done((f32[8,128]{1,0:T(8,128)S(1)}, f32[8,128]{1,0:T(8,128)S(1)}, u32[]{:S(2)}, u32[]{:S(2)}) %collective-permute-start.6) | collective-permute-done | bytes 4128 | tf_op jit(solution)/shard_map/ppermute | solution.py:415
  61.1 6.9 %collective-permute-done.7 = f32[8,128]{1,0:T(8,128)S(1)} collective-permute-done((f32[8,128]{1,0:T(8,128)S(1)}, f32[8,128]{1,0:T(8,128)S(1)}, u32[]{:S(2)}, u32[]{:S(2)}) %collective-permute-start.7) | collective-permute-done | bytes 4128 | tf_op jit(solution)/shard_map/ppermute | solution.py:415
  69.9 3.8 %forward_own_kernel.2.mid = f32[4,24,32,128]{3,2,1,0:T(8,128)S(1)} custom-call(f32[30,64,128]{2,1,0:T(8,128)S(1)} %get-tuple-element.54.own, bf16[256,512]{1,0:T(8,128)(2,1)S(1)} %copy-done.11, bf16[4,128,256]{2,1,0:T(8,128)(2,1)S(1)} %copy-done.14), custom_call_target="tpu_custom_call" | custom-call | flops 3221225472 | bytes 1000 | tf_op jit(solution)/shard_map/forward_own_kernel/pallas_call | solution.py:392
  73.9 7.6 %forward_kernel.2.blurred = f32[4,24,32,128]{3,2,1,0:T(8,128)S(1)} custom-call(f32[21,64,128]{2,1,0:T(8,128)} %collective-permute-done.12.x_a, f32[21,64,128]{2,1,0:T(8,128)} %collective-permute-done.13.x_b, f32[4,24,32,128]{3,2,1,0:T(8,128)S(1)} %forward_own_kernel.2.mid, bf16[256,512]{1,0:T(8,128)(2,1)S(1)} %copy-done.12, ...), custom_call_target="tpu_custom_call" | custom-call | flops 4294967296 | bytes 1000 | tf_op jit(solution)/shard_map/forward_kernel/pallas_call | solution.py:392
  81.4 7.4 %backward_kernel.2 = (f32[21,64,128]{2,1,0:T(8,128)S(1)}, f32[21,64,128]{2,1,0:T(8,128)S(1)}, f32[4,24,32,128]{3,2,1,0:T(8,128)S(1)}, f32[8,128]{1,0:T(8,128)S(1)}) custom-call(f32[8,128]{1,0:T(8,128)S(1)} %add.79.sums, s32[4]{0:T(128)S(1)} %copy-done.3, f32[1]{0:T(128)} %bitcast.norm, f32[4,24,32,128]{3,2,1,0:T(8,128)S(1)} %forward_kernel.2.blurred, ...), custom_call_target="tpu_custom_call" | custom-call | flops 4294967296 | bytes 1000 | tf_op jit(solution)/shard_map/backward_kernel/pallas_call | solution.py:392
  88.9 3.0 %collective-permute-start.15 = (f32[21,64,128]{2,1,0:T(8,128)S(1)}, f32[21,64,128]{2,1,0:T(8,128)S(1)}, u32[]{:S(2)}, u32[]{:S(2)}) collective-permute-start(f32[21,64,128]{2,1,0:T(8,128)S(1)} %get-tuple-element.63), channel_id=1, source_target_pairs={{16,32},{48,64},{80,96},{112,128},{144,160},{176,192},{208,224},{3... | collective-permute-start | bytes 2064392 | tf_op jit(solution)/shard_map/ppermute | solution.py:409
  91.9 3.5 %backward_own_kernel.2.own = f32[30,64,128]{2,1,0:T(8,128)S(1)} custom-call(f32[4,24,32,128]{3,2,1,0:T(8,128)S(1)} %get-tuple-element.61.mid, bf16[512,256]{1,0:T(8,128)(2,1)S(1)} %get-tuple-element.58.bz, bf16[4,256,128]{2,1,0:T(8,128)(2,1)S(1)} %copy-done.9), custom_call_target="tpu_custom_call" | custom-call | flops 3221225472 | bytes 1000 | tf_op jit(solution)/shard_map/backward_own_kernel/pallas_call | solution.py:392
  95.5 7.8 %collective-permute-done.15.x_b = f32[21,64,128]{2,1,0:T(8,128)S(1)} collective-permute-done((f32[21,64,128]{2,1,0:T(8,128)S(1)}, f32[21,64,128]{2,1,0:T(8,128)S(1)}, u32[]{:S(2)}, u32[]{:S(2)}) %collective-permute-start.15) | collective-permute-done | bytes 688160 | tf_op jit(solution)/shard_map/ppermute | solution.py:409
  104.3 3.4 %collective-permute-start.17 = (f32[30,16,128]{2,1,0:T(8,128)S(1)}, f32[30,16,128]{2,1,0:T(8,128)S(1)}, u32[]{:S(2)}, u32[]{:S(2)}) collective-permute-start(f32[30,16,128]{2,1,0:T(8,128)S(1)} %get-tuple-element.66), channel_id=1, source_target_pairs={{4,8},{8,4},{5,9},{9,5},{6,10},{10,6},{7,11},{11,7},{20,24},{24,20... | collective-permute-start | bytes 737288 | tf_op jit(solution)/shard_map/ppermute | solution.py:409
  107.6 2.7 %collective-permute-done.16.y_a = f32[30,16,128]{2,1,0:T(8,128)S(1)} collective-permute-done((f32[30,16,128]{2,1,0:T(8,128)S(1)}, f32[30,16,128]{2,1,0:T(8,128)S(1)}, u32[]{:S(2)}, u32[]{:S(2)}) %collective-permute-start.16) | collective-permute-done | bytes 245792 | tf_op jit(solution)/shard_map/ppermute | solution.py:409
  110.4 2.1 collective-permute-done.17.y_b
  112.7 2.9 %collective-permute-start.19 = (f32[3,32,128]{2,1,0:T(8,128)S(1)}, f32[3,32,128]{2,1,0:T(8,128)S(1)}, u32[]{:S(2)}, u32[]{:S(2)}) collective-permute-start(f32[3,32,128]{2,1,0:T(8,128)S(1)} %get-tuple-element.69), channel_id=1, source_target_pairs={{1,2},{2,1},{5,6},{6,5},{9,10},{10,9},{13,14},{14,13},{17,18},{18,... | collective-permute-start | bytes 147464 | tf_op jit(solution)/shard_map/ppermute | solution.py:409
  115.6 2.0 collective-permute-done.18.z_a
  117.6 3.1 %collective-permute-done.19.z_b = f32[3,32,128]{2,1,0:T(8,128)S(1)} collective-permute-done((f32[3,32,128]{2,1,0:T(8,128)S(1)}, f32[3,32,128]{2,1,0:T(8,128)S(1)}, u32[]{:S(2)}, u32[]{:S(2)}) %collective-permute-start.19) | collective-permute-done | bytes 49184 | tf_op jit(solution)/shard_map/ppermute | solution.py:409
  121.3 2.9 %collective-permute-start.29 = (f32[96,128]{1,0:T(8,128)S(1)}, f32[96,128]{1,0:T(8,128)S(1)}, u32[]{:S(2)}, u32[]{:S(2)}) collective-permute-start(f32[96,128]{1,0:T(8,128)S(1)} %get-tuple-element.74), channel_id=1, source_target_pairs={{1,2},{2,1},{5,6},{6,5},{9,10},{10,9},{13,14},{14,13},{17,18},{18,... | collective-permute-start | bytes 147464 | tf_op jit(solution)/shard_map/ppermute | solution.py:409
  124.3 2.0 collective-permute-done.28
  126.3 3.1 %collective-permute-done.29 = f32[96,128]{1,0:T(8,128)S(1)} collective-permute-done((f32[96,128]{1,0:T(8,128)S(1)}, f32[96,128]{1,0:T(8,128)S(1)}, u32[]{:S(2)}, u32[]{:S(2)}) %collective-permute-start.29) | collective-permute-done | bytes 49184 | tf_op jit(solution)/shard_map/ppermute | solution.py:409
  129.6 3.6 %collective-permute-start.31 = (f32[30,16,128]{2,1,0:T(8,128)S(1)}, f32[30,16,128]{2,1,0:T(8,128)S(1)}, u32[]{:S(2)}, u32[]{:S(2)}) collective-permute-start(f32[30,16,128]{2,1,0:T(8,128)S(1)} %get-tuple-element.76), channel_id=1, source_target_pairs={{4,8},{8,4},{5,9},{9,5},{6,10},{10,6},{7,11},{11,7},{20,24},{24,20... | collective-permute-start | bytes 737288 | tf_op jit(solution)/shard_map/ppermute | solution.py:409
  133.2 2.5 collective-permute-done.30.y_a
  135.8 1.9 collective-permute-done.31.y_b
  138.0 3.1 %collective-permute-start.33 = (f32[21,64,128]{2,1,0:T(8,128)S(1)}, f32[21,64,128]{2,1,0:T(8,128)S(1)}, u32[]{:S(2)}, u32[]{:S(2)}) collective-permute-start(f32[21,64,128]{2,1,0:T(8,128)S(1)} %get-tuple-element.78), channel_id=1, source_target_pairs={{16,32},{48,64},{80,96},{112,128},{144,160},{176,192},{208,224},{3... | collective-permute-start | bytes 2064392 | tf_op jit(solution)/shard_map/ppermute | solution.py:409
  141.2 1.2 collective-permute-done.20
  143.3 7.7 %collective-permute-done.21 = f32[8,128]{1,0:T(8,128)S(1)} collective-permute-done((f32[8,128]{1,0:T(8,128)S(1)}, f32[8,128]{1,0:T(8,128)S(1)}, u32[]{:S(2)}, u32[]{:S(2)}) %collective-permute-start.21) | collective-permute-done | bytes 4128 | tf_op jit(solution)/shard_map/ppermute | solution.py:415
  151.0 1.4 collective-permute-start.22
  152.4 3.7 %collective-permute-done.22 = f32[8,128]{1,0:T(8,128)S(1)} collective-permute-done((f32[8,128]{1,0:T(8,128)S(1)}, f32[8,128]{1,0:T(8,128)S(1)}, u32[]{:S(2)}, u32[]{:S(2)}) %collective-permute-start.22) | collective-permute-done | bytes 4128 | tf_op jit(solution)/shard_map/ppermute | solution.py:415
  156.1 3.6 %collective-permute-done.23 = f32[8,128]{1,0:T(8,128)S(1)} collective-permute-done((f32[8,128]{1,0:T(8,128)S(1)}, f32[8,128]{1,0:T(8,128)S(1)}, u32[]{:S(2)}, u32[]{:S(2)}) %collective-permute-start.23) | collective-permute-done | bytes 4128 | tf_op jit(solution)/shard_map/ppermute | solution.py:415
  159.7 10.7 %collective-permute-start.24 = (f32[8,128]{1,0:T(8,128)S(1)}, f32[8,128]{1,0:T(8,128)S(1)}, u32[]{:S(2)}, u32[]{:S(2)}) collective-permute-start(f32[8,128]{1,0:T(8,128)S(1)} %add.83), channel_id=1, source_target_pairs={{0,8},{4,12},{8,0},{12,4},{1,9},{5,13},{9,1},{13,5},{2,10},{6,14},... | collective-permute-start | bytes 12296 | tf_op jit(solution)/shard_map/ppermute | solution.py:415
  170.5 3.9 %collective-permute-done.24 = f32[8,128]{1,0:T(8,128)S(1)} collective-permute-done((f32[8,128]{1,0:T(8,128)S(1)}, f32[8,128]{1,0:T(8,128)S(1)}, u32[]{:S(2)}, u32[]{:S(2)}) %collective-permute-start.24) | collective-permute-done | bytes 4128 | tf_op jit(solution)/shard_map/ppermute | solution.py:415
  174.4 3.6 %collective-permute-done.25 = f32[8,128]{1,0:T(8,128)S(1)} collective-permute-done((f32[8,128]{1,0:T(8,128)S(1)}, f32[8,128]{1,0:T(8,128)S(1)}, u32[]{:S(2)}, u32[]{:S(2)}) %collective-permute-start.25) | collective-permute-done | bytes 4128 | tf_op jit(solution)/shard_map/ppermute | solution.py:415
  178.0 4.5 %collective-permute-done.26 = f32[8,128]{1,0:T(8,128)S(1)} collective-permute-done((f32[8,128]{1,0:T(8,128)S(1)}, f32[8,128]{1,0:T(8,128)S(1)}, u32[]{:S(2)}, u32[]{:S(2)}) %collective-permute-start.26) | collective-permute-done | bytes 4128 | tf_op jit(solution)/shard_map/ppermute | solution.py:415
  182.9 7.1 %collective-permute-done.27 = f32[8,128]{1,0:T(8,128)S(1)} collective-permute-done((f32[8,128]{1,0:T(8,128)S(1)}, f32[8,128]{1,0:T(8,128)S(1)}, u32[]{:S(2)}, u32[]{:S(2)}) %collective-permute-start.27) | collective-permute-done | bytes 4128 | tf_op jit(solution)/shard_map/ppermute | solution.py:415
  190.1 3.9 %forward_own_kernel.3.mid = f32[4,24,32,128]{3,2,1,0:T(8,128)S(1)} custom-call(f32[30,64,128]{2,1,0:T(8,128)S(1)} %get-tuple-element.79.own, bf16[256,512]{1,0:T(8,128)(2,1)S(1)} %copy-done.12, bf16[4,128,256]{2,1,0:T(8,128)(2,1)S(1)} %copy-done.14), custom_call_target="tpu_custom_call" | custom-call | flops 3221225472 | bytes 1000 | tf_op jit(solution)/shard_map/forward_own_kernel/pallas_call | solution.py:392
  193.9 6.2 %forward_kernel.3.blurred = f32[4,24,32,128]{3,2,1,0:T(8,128)S(1)} custom-call(f32[21,64,128]{2,1,0:T(8,128)S(1)} %collective-permute-done.32.x_a, f32[21,64,128]{2,1,0:T(8,128)S(1)} %collective-permute-done.33.x_b, f32[4,24,32,128]{3,2,1,0:T(8,128)S(1)} %forward_own_kernel.3.mid, bf16[256,512]{1,0:T(8,128)(2,1)S(1)} %copy-done.12, ...), custom_call_target="tpu_custom_call" | custom-call | flops 4294967296 | bytes 1000 | tf_op jit(solution)/shard_map/forward_kernel/pallas_call | solution.py:392
  200.1 7.4 %backward_kernel.3 = (f32[21,64,128]{2,1,0:T(8,128)S(1)}, f32[21,64,128]{2,1,0:T(8,128)S(1)}, f32[4,24,32,128]{3,2,1,0:T(8,128)S(1)}, f32[8,128]{1,0:T(8,128)S(1)}) custom-call(f32[8,128]{1,0:T(8,128)S(1)} %add_select_fusion.sums, s32[4]{0:T(128)S(1)} %copy-done.3, f32[1]{0:T(128)} %bitcast.norm, f32[4,24,32,128]{3,2,1,0:T(8,128)S(1)} %forward_kernel.3.blurred, ...), custom_call_target="tpu_custom_call" | custom-call | flops 4294967296 | bytes 1000 | tf_op jit(solution)/shard_map/backward_kernel/pallas_call | solution.py:392
  207.6 1.9 collective-permute-start.35
  210.9 2.0 collective-permute-start.41
  212.9 7.7 %collective-permute-done.41 = f32[8,128]{1,0:T(8,128)S(1)} collective-permute-done((f32[8,128]{1,0:T(8,128)S(1)}, f32[8,128]{1,0:T(8,128)S(1)}, u32[]{:S(2)}, u32[]{:S(2)}) %collective-permute-start.41) | collective-permute-done | bytes 4128 | tf_op jit(solution)/shard_map/ppermute | solution.py:415
  220.6 1.4 collective-permute-start.42
  222.0 3.5 %backward_own_kernel.3.own = f32[30,64,128]{2,1,0:T(8,128)S(1)} custom-call(f32[4,24,32,128]{3,2,1,0:T(8,128)S(1)} %get-tuple-element.80.mid, bf16[512,256]{1,0:T(8,128)(2,1)S(1)} %get-tuple-element.58.bz, bf16[4,256,128]{2,1,0:T(8,128)(2,1)S(1)} %copy-done.9), custom_call_target="tpu_custom_call" | custom-call | flops 3221225472 | bytes 1000 | tf_op jit(solution)/shard_map/backward_own_kernel/pallas_call | solution.py:392
  226.3 3.4 %collective-permute-start.37 = (f32[30,16,128]{2,1,0:T(8,128)S(1)}, f32[30,16,128]{2,1,0:T(8,128)S(1)}, u32[]{:S(2)}, u32[]{:S(2)}) collective-permute-start(f32[30,16,128]{2,1,0:T(8,128)S(1)} %get-tuple-element.85), channel_id=1, source_target_pairs={{4,8},{8,4},{5,9},{9,5},{6,10},{10,6},{7,11},{11,7},{20,24},{24,20... | collective-permute-start | bytes 737288 | tf_op jit(solution)/shard_map/ppermute | solution.py:409
  229.8 3.6 %collective-permute-done.43 = f32[8,128]{1,0:T(8,128)S(1)} collective-permute-done((f32[8,128]{1,0:T(8,128)S(1)}, f32[8,128]{1,0:T(8,128)S(1)}, u32[]{:S(2)}, u32[]{:S(2)}) %collective-permute-start.43) | collective-permute-done | bytes 4128 | tf_op jit(solution)/shard_map/ppermute | solution.py:415
  233.6 4.9 %collective-permute-done.44 = f32[8,128]{1,0:T(8,128)S(1)} collective-permute-done((f32[8,128]{1,0:T(8,128)S(1)}, f32[8,128]{1,0:T(8,128)S(1)}, u32[]{:S(2)}, u32[]{:S(2)}) %collective-permute-start.44) | collective-permute-done | bytes 4128 | tf_op jit(solution)/shard_map/ppermute | solution.py:415
  238.6 3.6 %collective-permute-done.45 = f32[8,128]{1,0:T(8,128)S(1)} collective-permute-done((f32[8,128]{1,0:T(8,128)S(1)}, f32[8,128]{1,0:T(8,128)S(1)}, u32[]{:S(2)}, u32[]{:S(2)}) %collective-permute-start.45) | collective-permute-done | bytes 4128 | tf_op jit(solution)/shard_map/ppermute | solution.py:415
  242.2 4.5 %collective-permute-done.46 = f32[8,128]{1,0:T(8,128)S(1)} collective-permute-done((f32[8,128]{1,0:T(8,128)S(1)}, f32[8,128]{1,0:T(8,128)S(1)}, u32[]{:S(2)}, u32[]{:S(2)}) %collective-permute-start.46) | collective-permute-done | bytes 4128 | tf_op jit(solution)/shard_map/ppermute | solution.py:415
  246.7 7.5 %collective-permute-done.47 = f32[8,128]{1,0:T(8,128)S(1)} collective-permute-done((f32[8,128]{1,0:T(8,128)S(1)}, f32[8,128]{1,0:T(8,128)S(1)}, u32[]{:S(2)}, u32[]{:S(2)}) %collective-permute-start.47) | collective-permute-done | bytes 4128 | tf_op jit(solution)/shard_map/ppermute | solution.py:415
  254.6 2.4 collective-permute-start.39
  257.6 1.9 collective-permute-done.38.z_a
  259.5 3.1 %collective-permute-done.39.z_b = f32[3,32,128]{2,1,0:T(8,128)S(1)} collective-permute-done((f32[3,32,128]{2,1,0:T(8,128)S(1)}, f32[3,32,128]{2,1,0:T(8,128)S(1)}, u32[]{:S(2)}, u32[]{:S(2)}) %collective-permute-start.39) | collective-permute-done | bytes 49184 | tf_op jit(solution)/shard_map/ppermute | solution.py:409
  (116 shorter events, 16.9 us)
Async XLA Ops:
  0.6 1.0 copy-start
  1.9 5.1 %collective-permute-start.8 = (f32[96,128]{1,0:T(8,128)S(1)}, f32[96,128]{1,0:T(8,128)S(1)}, u32[]{:S(2)}, u32[]{:S(2)}) collective-permute-start(f32[96,128]{1,0:T(8,128)S(1)} %get-tuple-element.48), channel_id=1, source_target_pairs={{0,1},{1,0},{2,3},{3,2},{4,5},{5,4},{6,7},{7,6},{8,9},{9,8},{10,11... | collective-permute-start | bytes 147464 | tf_op jit(solution)/shard_map/ppermute | solution.py:409
  3.4 8.6 %collective-permute-start.9 = (f32[96,128]{1,0:T(8,128)S(1)}, f32[96,128]{1,0:T(8,128)S(1)}, u32[]{:S(2)}, u32[]{:S(2)}) collective-permute-start(f32[96,128]{1,0:T(8,128)S(1)} %get-tuple-element.49), channel_id=1, source_target_pairs={{1,2},{2,1},{5,6},{6,5},{9,10},{10,9},{13,14},{14,13},{17,18},{18,... | collective-permute-start | bytes 147464 | tf_op jit(solution)/shard_map/ppermute | solution.py:409
  12.1 6.3 %collective-permute-start.10 = (f32[30,16,128]{2,1,0:T(8,128)S(1)}, f32[30,16,128]{2,1,0:T(8,128)S(1)}, u32[]{:S(2)}, u32[]{:S(2)}) collective-permute-start(f32[30,16,128]{2,1,0:T(8,128)S(1)} %get-tuple-element.50), channel_id=1, source_target_pairs={{0,4},{4,0},{8,12},{12,8},{1,5},{5,1},{9,13},{13,9},{2,6},{6,2},{1... | collective-permute-start | bytes 737288 | tf_op jit(solution)/shard_map/ppermute | solution.py:409
  12.6 8.5 %collective-permute-start.11 = (f32[30,16,128]{2,1,0:T(8,128)S(1)}, f32[30,16,128]{2,1,0:T(8,128)S(1)}, u32[]{:S(2)}, u32[]{:S(2)}) collective-permute-start(f32[30,16,128]{2,1,0:T(8,128)S(1)} %get-tuple-element.51), channel_id=1, source_target_pairs={{4,8},{8,4},{5,9},{9,5},{6,10},{10,6},{7,11},{11,7},{20,24},{24,20... | collective-permute-start | bytes 737288 | tf_op jit(solution)/shard_map/ppermute | solution.py:409
  22.4 51.4 %collective-permute-start.12 = (f32[21,64,128]{2,1,0:T(8,128)}, f32[21,64,128]{2,1,0:T(8,128)}, u32[]{:S(2)}, u32[]{:S(2)}) collective-permute-start(f32[21,64,128]{2,1,0:T(8,128)} %get-tuple-element.52), channel_id=1, source_target_pairs={{0,16},{16,0},{32,48},{48,32},{64,80},{80,64},{96,112},{112,96},{1... | collective-permute-start | bytes 2064392 | tf_op jit(solution)/shard_map/ppermute | solution.py:409
  22.4 9.8 %copy-start.1 = (f32[24,32,128]{2,1,0:T(8,128)S(1)}, f32[24,32,128]{2,1,0:T(8,128)}, u32[]{:S(2)}) copy-start(f32[24,32,128]{2,1,0:T(8,128)} %est.9) | copy-start | bytes 1179652
  22.4 9.8 %copy-start.2 = (f32[4,24,32,128]{3,2,1,0:T(8,128)S(1)}, f32[4,24,32,128]{3,2,1,0:T(8,128)}, u32[]{:S(2)}) copy-start(f32[4,24,32,128]{3,2,1,0:T(8,128)} %views.5) | copy-start | bytes 4718596
  22.4 51.4 %collective-permute-start.13 = (f32[21,64,128]{2,1,0:T(8,128)}, f32[21,64,128]{2,1,0:T(8,128)}, u32[]{:S(2)}, u32[]{:S(2)}) collective-permute-start(f32[21,64,128]{2,1,0:T(8,128)} %get-tuple-element.53), channel_id=1, source_target_pairs={{16,32},{48,64},{80,96},{112,128},{144,160},{176,192},{208,224},{3... | collective-permute-start | bytes 2064392 | tf_op jit(solution)/shard_map/ppermute | solution.py:409
  32.1 0.9 copy-start.4
  32.1 1.2 copy-start.6
  32.1 1.2 copy-start.8
  32.1 1.3 copy-start.10
  32.1 1.4 copy-start.13
  32.2 23.6 %copy-start.15 = (s32[4,3,31]{2,0,1:T(4,128)S(1)}, s32[4,3,31]{2,0,1:T(4,128)}, u32[]{:S(2)}) copy-start(s32[4,3,31]{2,0,1:T(4,128)} %param.6) | copy-start | bytes 4468
  32.2 28.3 %copy-start.3 = (s32[4]{0:T(128)S(1)}, s32[4]{0:T(128)}, u32[]{:S(2)}) copy-start(s32[4]{0:T(128)} %weights.3) | copy-start | bytes 52
  33.5 1.2 collective-permute-start
  34.7 3.6 %collective-permute-start.1 = (f32[8,128]{1,0:T(8,128)S(1)}, f32[8,128]{1,0:T(8,128)S(1)}, u32[]{:S(2)}, u32[]{:S(2)}) collective-permute-start(f32[8,128]{1,0:T(8,128)S(1)} %add.72), channel_id=1, source_target_pairs={{0,32},{32,0},{64,96},{96,64},{1,33},{33,1},{65,97},{97,65},{2,34}... | collective-permute-start | bytes 12296 | tf_op jit(solution)/shard_map/ppermute | solution.py:415
  38.3 5.1 %collective-permute-start.2 = (f32[8,128]{1,0:T(8,128)S(1)}, f32[8,128]{1,0:T(8,128)S(1)}, u32[]{:S(2)}, u32[]{:S(2)}) collective-permute-start(f32[8,128]{1,0:T(8,128)S(1)} %add.73), channel_id=1, source_target_pairs={{0,64},{32,96},{64,0},{96,32},{1,65},{33,97},{65,1},{97,33},{2,66}... | collective-permute-start | bytes 12296 | tf_op jit(solution)/shard_map/ppermute | solution.py:415
  43.4 3.6 %collective-permute-start.3 = (f32[8,128]{1,0:T(8,128)S(1)}, f32[8,128]{1,0:T(8,128)S(1)}, u32[]{:S(2)}, u32[]{:S(2)}) collective-permute-start(f32[8,128]{1,0:T(8,128)S(1)} %add.74), channel_id=1, source_target_pairs={{0,4},{4,0},{8,12},{12,8},{1,5},{5,1},{9,13},{13,9},{2,6},{6,2},{1... | collective-permute-start | bytes 12296 | tf_op jit(solution)/shard_map/ppermute | solution.py:415
  47.0 5.1 %collective-permute-start.4 = (f32[8,128]{1,0:T(8,128)S(1)}, f32[8,128]{1,0:T(8,128)S(1)}, u32[]{:S(2)}, u32[]{:S(2)}) collective-permute-start(f32[8,128]{1,0:T(8,128)S(1)} %add.75), channel_id=1, source_target_pairs={{0,8},{4,12},{8,0},{12,4},{1,9},{5,13},{9,1},{13,5},{2,10},{6,14},... | collective-permute-start | bytes 12296 | tf_op jit(solution)/shard_map/ppermute | solution.py:415
  52.2 3.6 %collective-permute-start.5 = (f32[8,128]{1,0:T(8,128)S(1)}, f32[8,128]{1,0:T(8,128)S(1)}, u32[]{:S(2)}, u32[]{:S(2)}) collective-permute-start(f32[8,128]{1,0:T(8,128)S(1)} %add.76), channel_id=1, source_target_pairs={{0,128},{128,0},{1,129},{129,1},{2,130},{130,2},{3,131},{131,3},{4... | collective-permute-start | bytes 12296 | tf_op jit(solution)/shard_map/ppermute | solution.py:415
  55.8 4.5 %collective-permute-start.6 = (f32[8,128]{1,0:T(8,128)S(1)}, f32[8,128]{1,0:T(8,128)S(1)}, u32[]{:S(2)}, u32[]{:S(2)}) collective-permute-start(f32[8,128]{1,0:T(8,128)S(1)} %add.77), channel_id=1, source_target_pairs={{0,1},{1,0},{2,3},{3,2},{4,5},{5,4},{6,7},{7,6},{8,9},{9,8},{10,11... | collective-permute-start | bytes 12296 | tf_op jit(solution)/shard_map/ppermute | solution.py:415
  60.3 7.8 %collective-permute-start.7 = (f32[8,128]{1,0:T(8,128)S(1)}, f32[8,128]{1,0:T(8,128)S(1)}, u32[]{:S(2)}, u32[]{:S(2)}) collective-permute-start(f32[8,128]{1,0:T(8,128)S(1)} %add.78), channel_id=1, source_target_pairs={{0,2},{1,3},{2,0},{3,1},{4,6},{5,7},{6,4},{7,5},{8,10},{9,11},{10,... | collective-permute-start | bytes 12296 | tf_op jit(solution)/shard_map/ppermute | solution.py:415
  68.0 1.0 copy-start.11
  69.0 0.9 copy-start.14
  69.9 3.9 %copy-start.5 = (bf16[4,192,432]{2,1,0:T(8,128)(2,1)S(1)}, bf16[4,192,432]{2,1,0:T(8,128)(2,1)}, u32[]{:S(2)}) copy-start(bf16[4,192,432]{2,1,0:T(8,128)(2,1)} %copy-done.4) | copy-start | bytes 1990660
  69.9 3.9 %copy-start.12 = (bf16[256,512]{1,0:T(8,128)(2,1)S(1)}, bf16[256,512]{1,0:T(8,128)(2,1)}, u32[]{:S(2)}) copy-start(bf16[256,512]{1,0:T(8,128)(2,1)} %copy-done.10) | copy-start | bytes 786436
  73.8 7.6 %copy-start.7 = (bf16[4,432,192]{2,1,0:T(8,128)(2,1)S(1)}, bf16[4,432,192]{2,1,0:T(8,128)(2,1)}, u32[]{:S(2)}) copy-start(bf16[4,432,192]{2,1,0:T(8,128)(2,1)} %copy-done.6) | copy-start | bytes 1990660
  73.8 7.6 %copy-start.9 = (bf16[4,256,128]{2,1,0:T(8,128)(2,1)S(1)}, bf16[4,256,128]{2,1,0:T(8,128)(2,1)}, u32[]{:S(2)}) copy-start(bf16[4,256,128]{2,1,0:T(8,128)(2,1)} %copy-done.8) | copy-start | bytes 786436
  88.8 6.6 %collective-permute-start.14 = (f32[21,64,128]{2,1,0:T(8,128)S(1)}, f32[21,64,128]{2,1,0:T(8,128)S(1)}, u32[]{:S(2)}, u32[]{:S(2)}) collective-permute-start(f32[21,64,128]{2,1,0:T(8,128)S(1)} %get-tuple-element.62), channel_id=1, source_target_pairs={{0,16},{16,0},{32,48},{48,32},{64,80},{80,64},{96,112},{112,96},{1... | collective-permute-start | bytes 2064392 | tf_op jit(solution)/shard_map/ppermute | solution.py:409
  88.9 14.4 %collective-permute-start.15 = (f32[21,64,128]{2,1,0:T(8,128)S(1)}, f32[21,64,128]{2,1,0:T(8,128)S(1)}, u32[]{:S(2)}, u32[]{:S(2)}) collective-permute-start(f32[21,64,128]{2,1,0:T(8,128)S(1)} %get-tuple-element.63), channel_id=1, source_target_pairs={{16,32},{48,64},{80,96},{112,128},{144,160},{176,192},{208,224},{3... | collective-permute-start | bytes 2064392 | tf_op jit(solution)/shard_map/ppermute | solution.py:409
  103.8 6.6 %collective-permute-start.16 = (f32[30,16,128]{2,1,0:T(8,128)S(1)}, f32[30,16,128]{2,1,0:T(8,128)S(1)}, u32[]{:S(2)}, u32[]{:S(2)}) collective-permute-start(f32[30,16,128]{2,1,0:T(8,128)S(1)} %get-tuple-element.65), channel_id=1, source_target_pairs={{0,4},{4,0},{8,12},{12,8},{1,5},{5,1},{9,13},{13,9},{2,6},{6,2},{1... | collective-permute-start | bytes 737288 | tf_op jit(solution)/shard_map/ppermute | solution.py:409
  104.3 8.2 %collective-permute-start.17 = (f32[30,16,128]{2,1,0:T(8,128)S(1)}, f32[30,16,128]{2,1,0:T(8,128)S(1)}, u32[]{:S(2)}, u32[]{:S(2)}) collective-permute-start(f32[30,16,128]{2,1,0:T(8,128)S(1)} %get-tuple-element.66), channel_id=1, source_target_pairs={{4,8},{8,4},{5,9},{9,5},{6,10},{10,6},{7,11},{11,7},{20,24},{24,20... | collective-permute-start | bytes 737288 | tf_op jit(solution)/shard_map/ppermute | solution.py:409
  112.6 5.1 %collective-permute-start.18 = (f32[3,32,128]{2,1,0:T(8,128)S(1)}, f32[3,32,128]{2,1,0:T(8,128)S(1)}, u32[]{:S(2)}, u32[]{:S(2)}) collective-permute-start(f32[3,32,128]{2,1,0:T(8,128)S(1)} %get-tuple-element.68), channel_id=1, source_target_pairs={{0,1},{1,0},{2,3},{3,2},{4,5},{5,4},{6,7},{7,6},{8,9},{9,8},{10,11... | collective-permute-start | bytes 147464 | tf_op jit(solution)/shard_map/ppermute | solution.py:409
  112.7 8.1 %collective-permute-start.19 = (f32[3,32,128]{2,1,0:T(8,128)S(1)}, f32[3,32,128]{2,1,0:T(8,128)S(1)}, u32[]{:S(2)}, u32[]{:S(2)}) collective-permute-start(f32[3,32,128]{2,1,0:T(8,128)S(1)} %get-tuple-element.69), channel_id=1, source_target_pairs={{1,2},{2,1},{5,6},{6,5},{9,10},{10,9},{13,14},{14,13},{17,18},{18,... | collective-permute-start | bytes 147464 | tf_op jit(solution)/shard_map/ppermute | solution.py:409
  121.2 5.1 %collective-permute-start.28 = (f32[96,128]{1,0:T(8,128)S(1)}, f32[96,128]{1,0:T(8,128)S(1)}, u32[]{:S(2)}, u32[]{:S(2)}) collective-permute-start(f32[96,128]{1,0:T(8,128)S(1)} %get-tuple-element.73), channel_id=1, source_target_pairs={{0,1},{1,0},{2,3},{3,2},{4,5},{5,4},{6,7},{7,6},{8,9},{9,8},{10,11... | collective-permute-start | bytes 147464 | tf_op jit(solution)/shard_map/ppermute | solution.py:409
  121.3 8.1 %collective-permute-start.29 = (f32[96,128]{1,0:T(8,128)S(1)}, f32[96,128]{1,0:T(8,128)S(1)}, u32[]{:S(2)}, u32[]{:S(2)}) collective-permute-start(f32[96,128]{1,0:T(8,128)S(1)} %get-tuple-element.74), channel_id=1, source_target_pairs={{1,2},{2,1},{5,6},{6,5},{9,10},{10,9},{13,14},{14,13},{17,18},{18,... | collective-permute-start | bytes 147464 | tf_op jit(solution)/shard_map/ppermute | solution.py:409
  129.5 6.3 %collective-permute-start.30 = (f32[30,16,128]{2,1,0:T(8,128)S(1)}, f32[30,16,128]{2,1,0:T(8,128)S(1)}, u32[]{:S(2)}, u32[]{:S(2)}) collective-permute-start(f32[30,16,128]{2,1,0:T(8,128)S(1)} %get-tuple-element.75), channel_id=1, source_target_pairs={{0,4},{4,0},{8,12},{12,8},{1,5},{5,1},{9,13},{13,9},{2,6},{6,2},{1... | collective-permute-start | bytes 737288 | tf_op jit(solution)/shard_map/ppermute | solution.py:409
  129.6 8.1 %collective-permute-start.31 = (f32[30,16,128]{2,1,0:T(8,128)S(1)}, f32[30,16,128]{2,1,0:T(8,128)S(1)}, u32[]{:S(2)}, u32[]{:S(2)}) collective-permute-start(f32[30,16,128]{2,1,0:T(8,128)S(1)} %get-tuple-element.76), channel_id=1, source_target_pairs={{4,8},{8,4},{5,9},{9,5},{6,10},{10,6},{7,11},{11,7},{20,24},{24,20... | collective-permute-start | bytes 737288 | tf_op jit(solution)/shard_map/ppermute | solution.py:409
  137.9 56.0 %collective-permute-start.32 = (f32[21,64,128]{2,1,0:T(8,128)S(1)}, f32[21,64,128]{2,1,0:T(8,128)S(1)}, u32[]{:S(2)}, u32[]{:S(2)}) collective-permute-start(f32[21,64,128]{2,1,0:T(8,128)S(1)} %get-tuple-element.77), channel_id=1, source_target_pairs={{0,16},{16,0},{32,48},{48,32},{64,80},{80,64},{96,112},{112,96},{1... | collective-permute-start | bytes 2064392 | tf_op jit(solution)/shard_map/ppermute | solution.py:409
  138.0 55.9 %collective-permute-start.33 = (f32[21,64,128]{2,1,0:T(8,128)S(1)}, f32[21,64,128]{2,1,0:T(8,128)S(1)}, u32[]{:S(2)}, u32[]{:S(2)}) collective-permute-start(f32[21,64,128]{2,1,0:T(8,128)S(1)} %get-tuple-element.78), channel_id=1, source_target_pairs={{16,32},{48,64},{80,96},{112,128},{144,160},{176,192},{208,224},{3... | collective-permute-start | bytes 2064392 | tf_op jit(solution)/shard_map/ppermute | solution.py:409
  141.1 1.3 collective-permute-start.20
  142.4 8.6 %collective-permute-start.21 = (f32[8,128]{1,0:T(8,128)S(1)}, f32[8,128]{1,0:T(8,128)S(1)}, u32[]{:S(2)}, u32[]{:S(2)}) collective-permute-start(f32[8,128]{1,0:T(8,128)S(1)} %add.80), channel_id=1, source_target_pairs={{0,32},{32,0},{64,96},{96,64},{1,33},{33,1},{65,97},{97,65},{2,34}... | collective-permute-start | bytes 12296 | tf_op jit(solution)/shard_map/ppermute | solution.py:415
  151.0 5.1 %collective-permute-start.22 = (f32[8,128]{1,0:T(8,128)S(1)}, f32[8,128]{1,0:T(8,128)S(1)}, u32[]{:S(2)}, u32[]{:S(2)}) collective-permute-start(f32[8,128]{1,0:T(8,128)S(1)} %add.81), channel_id=1, source_target_pairs={{0,64},{32,96},{64,0},{96,32},{1,65},{33,97},{65,1},{97,33},{2,66}... | collective-permute-start | bytes 12296 | tf_op jit(solution)/shard_map/ppermute | solution.py:415
  156.1 3.6 %collective-permute-start.23 = (f32[8,128]{1,0:T(8,128)S(1)}, f32[8,128]{1,0:T(8,128)S(1)}, u32[]{:S(2)}, u32[]{:S(2)}) collective-permute-start(f32[8,128]{1,0:T(8,128)S(1)} %add.82), channel_id=1, source_target_pairs={{0,4},{4,0},{8,12},{12,8},{1,5},{5,1},{9,13},{13,9},{2,6},{6,2},{1... | collective-permute-start | bytes 12296 | tf_op jit(solution)/shard_map/ppermute | solution.py:415
  159.7 14.7 %collective-permute-start.24 = (f32[8,128]{1,0:T(8,128)S(1)}, f32[8,128]{1,0:T(8,128)S(1)}, u32[]{:S(2)}, u32[]{:S(2)}) collective-permute-start(f32[8,128]{1,0:T(8,128)S(1)} %add.83), channel_id=1, source_target_pairs={{0,8},{4,12},{8,0},{12,4},{1,9},{5,13},{9,1},{13,5},{2,10},{6,14},... | collective-permute-start | bytes 12296 | tf_op jit(solution)/shard_map/ppermute | solution.py:415
  174.4 3.6 %collective-permute-start.25 = (f32[8,128]{1,0:T(8,128)S(1)}, f32[8,128]{1,0:T(8,128)S(1)}, u32[]{:S(2)}, u32[]{:S(2)}) collective-permute-start(f32[8,128]{1,0:T(8,128)S(1)} %add.84), channel_id=1, source_target_pairs={{0,128},{128,0},{1,129},{129,1},{2,130},{130,2},{3,131},{131,3},{4... | collective-permute-start | bytes 12296 | tf_op jit(solution)/shard_map/ppermute | solution.py:415
  178.0 4.5 %collective-permute-start.26 = (f32[8,128]{1,0:T(8,128)S(1)}, f32[8,128]{1,0:T(8,128)S(1)}, u32[]{:S(2)}, u32[]{:S(2)}) collective-permute-start(f32[8,128]{1,0:T(8,128)S(1)} %add.85), channel_id=1, source_target_pairs={{0,1},{1,0},{2,3},{3,2},{4,5},{5,4},{6,7},{7,6},{8,9},{9,8},{10,11... | collective-permute-start | bytes 12296 | tf_op jit(solution)/shard_map/ppermute | solution.py:415
  182.5 7.5 %collective-permute-start.27 = (f32[8,128]{1,0:T(8,128)S(1)}, f32[8,128]{1,0:T(8,128)S(1)}, u32[]{:S(2)}, u32[]{:S(2)}) collective-permute-start(f32[8,128]{1,0:T(8,128)S(1)} %add.86), channel_id=1, source_target_pairs={{0,2},{1,3},{2,0},{3,1},{4,6},{5,7},{6,4},{7,5},{8,10},{9,11},{10,... | collective-permute-start | bytes 12296 | tf_op jit(solution)/shard_map/ppermute | solution.py:415
  207.5 18.0 %collective-permute-start.34 = (f32[21,64,128]{2,1,0:T(8,128)S(1)}, f32[21,64,128]{2,1,0:T(8,128)S(1)}, u32[]{:S(2)}, u32[]{:S(2)}) collective-permute-start(f32[21,64,128]{2,1,0:T(8,128)S(1)} %get-tuple-element.81), channel_id=1, source_target_pairs={{0,16},{16,0},{32,48},{48,32},{64,80},{80,64},{96,112},{112,96},{1... | collective-permute-start | bytes 2064392 | tf_op jit(solution)/shard_map/ppermute | solution.py:409
  207.6 17.9 %collective-permute-start.35 = (f32[21,64,128]{2,1,0:T(8,128)S(1)}, f32[21,64,128]{2,1,0:T(8,128)S(1)}, u32[]{:S(2)}, u32[]{:S(2)}) collective-permute-start(f32[21,64,128]{2,1,0:T(8,128)S(1)} %get-tuple-element.82), channel_id=1, source_target_pairs={{16,32},{48,64},{80,96},{112,128},{144,160},{176,192},{208,224},{3... | collective-permute-start | bytes 2064392 | tf_op jit(solution)/shard_map/ppermute | solution.py:409
  209.5 1.4 collective-permute-start.40
  210.9 9.7 %collective-permute-start.41 = (f32[8,128]{1,0:T(8,128)S(1)}, f32[8,128]{1,0:T(8,128)S(1)}, u32[]{:S(2)}, u32[]{:S(2)}) collective-permute-start(f32[8,128]{1,0:T(8,128)S(1)} %add.88), channel_id=1, source_target_pairs={{0,32},{32,0},{64,96},{96,64},{1,33},{33,1},{65,97},{97,65},{2,34}... | collective-permute-start | bytes 12296 | tf_op jit(solution)/shard_map/ppermute | solution.py:415
  220.6 9.1 %collective-permute-start.42 = (f32[8,128]{1,0:T(8,128)S(1)}, f32[8,128]{1,0:T(8,128)S(1)}, u32[]{:S(2)}, u32[]{:S(2)}) collective-permute-start(f32[8,128]{1,0:T(8,128)S(1)} %add.89), channel_id=1, source_target_pairs={{0,64},{32,96},{64,0},{96,32},{1,65},{33,97},{65,1},{97,33},{2,66}... | collective-permute-start | bytes 12296 | tf_op jit(solution)/shard_map/ppermute | solution.py:415
  226.0 28.3 %collective-permute-start.36 = (f32[30,16,128]{2,1,0:T(8,128)S(1)}, f32[30,16,128]{2,1,0:T(8,128)S(1)}, u32[]{:S(2)}, u32[]{:S(2)}) collective-permute-start(f32[30,16,128]{2,1,0:T(8,128)S(1)} %get-tuple-element.84), channel_id=1, source_target_pairs={{0,4},{4,0},{8,12},{12,8},{1,5},{5,1},{9,13},{13,9},{2,6},{6,2},{1... | collective-permute-start | bytes 737288 | tf_op jit(solution)/shard_map/ppermute | solution.py:409
  226.3 27.9 %collective-permute-start.37 = (f32[30,16,128]{2,1,0:T(8,128)S(1)}, f32[30,16,128]{2,1,0:T(8,128)S(1)}, u32[]{:S(2)}, u32[]{:S(2)}) collective-permute-start(f32[30,16,128]{2,1,0:T(8,128)S(1)} %get-tuple-element.85), channel_id=1, source_target_pairs={{4,8},{8,4},{5,9},{9,5},{6,10},{10,6},{7,11},{11,7},{20,24},{24,20... | collective-permute-start | bytes 737288 | tf_op jit(solution)/shard_map/ppermute | solution.py:409
  229.7 3.7 %collective-permute-start.43 = (f32[8,128]{1,0:T(8,128)S(1)}, f32[8,128]{1,0:T(8,128)S(1)}, u32[]{:S(2)}, u32[]{:S(2)}) collective-permute-start(f32[8,128]{1,0:T(8,128)S(1)} %add.90), channel_id=1, source_target_pairs={{0,4},{4,0},{8,12},{12,8},{1,5},{5,1},{9,13},{13,9},{2,6},{6,2},{1... | collective-permute-start | bytes 12296 | tf_op jit(solution)/shard_map/ppermute | solution.py:415
  233.4 5.1 %collective-permute-start.44 = (f32[8,128]{1,0:T(8,128)S(1)}, f32[8,128]{1,0:T(8,128)S(1)}, u32[]{:S(2)}, u32[]{:S(2)}) collective-permute-start(f32[8,128]{1,0:T(8,128)S(1)} %add.91), channel_id=1, source_target_pairs={{0,8},{4,12},{8,0},{12,4},{1,9},{5,13},{9,1},{13,5},{2,10},{6,14},... | collective-permute-start | bytes 12296 | tf_op jit(solution)/shard_map/ppermute | solution.py:415
  238.6 3.6 %collective-permute-start.45 = (f32[8,128]{1,0:T(8,128)S(1)}, f32[8,128]{1,0:T(8,128)S(1)}, u32[]{:S(2)}, u32[]{:S(2)}) collective-permute-start(f32[8,128]{1,0:T(8,128)S(1)} %add.92), channel_id=1, source_target_pairs={{0,128},{128,0},{1,129},{129,1},{2,130},{130,2},{3,131},{131,3},{4... | collective-permute-start | bytes 12296 | tf_op jit(solution)/shard_map/ppermute | solution.py:415
  242.2 4.5 %collective-permute-start.46 = (f32[8,128]{1,0:T(8,128)S(1)}, f32[8,128]{1,0:T(8,128)S(1)}, u32[]{:S(2)}, u32[]{:S(2)}) collective-permute-start(f32[8,128]{1,0:T(8,128)S(1)} %add.93), channel_id=1, source_target_pairs={{0,1},{1,0},{2,3},{3,2},{4,5},{5,4},{6,7},{7,6},{8,9},{9,8},{10,11... | collective-permute-start | bytes 12296 | tf_op jit(solution)/shard_map/ppermute | solution.py:415
  246.7 7.5 %collective-permute-start.47 = (f32[8,128]{1,0:T(8,128)S(1)}, f32[8,128]{1,0:T(8,128)S(1)}, u32[]{:S(2)}, u32[]{:S(2)}) collective-permute-start(f32[8,128]{1,0:T(8,128)S(1)} %add.94), channel_id=1, source_target_pairs={{0,2},{1,3},{2,0},{3,1},{4,6},{5,7},{6,4},{7,5},{8,10},{9,11},{10,... | collective-permute-start | bytes 12296 | tf_op jit(solution)/shard_map/ppermute | solution.py:415
  254.4 5.1 %collective-permute-start.38 = (f32[3,32,128]{2,1,0:T(8,128)S(1)}, f32[3,32,128]{2,1,0:T(8,128)S(1)}, u32[]{:S(2)}, u32[]{:S(2)}) collective-permute-start(f32[3,32,128]{2,1,0:T(8,128)S(1)} %get-tuple-element.87), channel_id=1, source_target_pairs={{0,1},{1,0},{2,3},{3,2},{4,5},{5,4},{6,7},{7,6},{8,9},{9,8},{10,11... | collective-permute-start | bytes 147464 | tf_op jit(solution)/shard_map/ppermute | solution.py:409
  254.6 8.1 %collective-permute-start.39 = (f32[3,32,128]{2,1,0:T(8,128)S(1)}, f32[3,32,128]{2,1,0:T(8,128)S(1)}, u32[]{:S(2)}, u32[]{:S(2)}) collective-permute-start(f32[3,32,128]{2,1,0:T(8,128)S(1)} %get-tuple-element.88), channel_id=1, source_target_pairs={{1,2},{2,1},{5,6},{6,5},{9,10},{10,9},{13,14},{14,13},{17,18},{18,... | collective-permute-start | bytes 147464 | tf_op jit(solution)/shard_map/ppermute | solution.py:409
